TPU v7x, 32 devices: a whole 2x2x4 slice. The times are simulated.
32 devices in a mesh: section: 4 (over y, core), dp: 8 (over z, x).
Axes of the slice: x: 2, y: 2, z: 4, core: 2. Of those that a mesh axis runs over, the one named last changes fastest.
Arguments:
- inputs: bfloat16 [1536, 4096], P('dp'), may hold values from -6 to 6
- output_cotangent: bfloat16 [1536, 4096], P('dp'), may hold values from -6 to 6
- lengths: int32 [16], P('dp'), may hold values from 24 to 96
- query_examples: int32 [16], replicated, may hold values from 0 to 15
- norm_gain: bfloat16 [4, 4096], P('section'), may hold values from 0.5 to 1.5
- value_weight: bfloat16 [4, 4096, 1024], P('section', 'dp'), may hold values from -0.09375 to 0.09375
- output_weight: bfloat16 [4, 4096, 1024], P('section', 'dp'), may hold values from -0.1875 to 0.1875
- input_projection: bfloat16 [4, 32, 4096], P('section'), may hold values from -0.09375 to 0.09375
- output_projection: bfloat16 [4, 32, 1024], P('section'), may hold values from -0.1875 to 0.1875
- fisher_prior: float32 [4, 1024, 1024], P('section'), as said below
Outputs:
- scores: float32 [16, 16], P('dp')
Inputs may be any that keep to these rules, and one draw needn't show every extreme that they name: `fisher_prior`: each block's 1024 x 1024 matrix is symmetric and positive definite.
All inputs are finite; a program needn't handle non-finite values.
Results may differ from a plain program's by a relative error of at most 0.0013.
Values may be sent and summed in bfloat16 or wider, within the bound.
A program may use at most 128 MiB of HBM per device.

v0:
```python
import functools

import jax
import jax.numpy as jnp
from jax import lax
from jax.experimental import pallas as pl
from jax.experimental.pallas import tpu as pltpu
from jax.sharding import PartitionSpec as P


HIGHEST = lax.Precision.HIGHEST


def inverted(block):
    size = block.shape[0]
    rows = lax.broadcasted_iota(jnp.int32, block.shape, 0)
    columns = lax.broadcasted_iota(jnp.int32, block.shape, 1)

    def sweep(pivot, held):
        at_row, at_column = rows == pivot, columns == pivot
        row = jnp.sum(jnp.where(at_row, held, 0.0), axis=0, keepdims=True)
        column = jnp.sum(jnp.where(at_column, held, 0.0), axis=1, keepdims=True)
        corner = jnp.sum(jnp.where(at_column[:1], row, 0.0), axis=1, keepdims=True)
        scale = 1.0 / corner
        scaled = row * scale
        updated = held - column * scaled
        updated = jnp.where(at_row, scaled, updated)
        updated = jnp.where(at_column, column * scale, updated)
        return jnp.where(at_row & at_column, -scale, updated)

    return -lax.fori_loop(0, size, sweep, block)


def sweep_strip(work, strip, step, block):
    span = pl.ds(pl.multiple_of(step * block, block), block)
    corner = inverted(work[span, span])
    strip[...] = jnp.dot(
        corner, work[span, :], precision=HIGHEST, preferred_element_type=jnp.float32
    )
    strip[:, span] = -corner


def sweep_rest(work, strip, step, block):
    span = pl.ds(pl.multiple_of(step * block, block), block)

    @pl.loop(0, work.shape[0] // block)
    def _(other):
        across = pl.ds(pl.multiple_of(other * block, block), block)

        @pl.when(other != step)
        def _():
            work[across, :] -= jnp.dot(
                work[span, across].T, strip[...], precision=HIGHEST,
                preferred_element_type=jnp.float32,
            )
            work[across, span] = strip[:, across].T

    work[span, :] = strip[...]


def ring_device(place, count):
    if count % 4 or count < 8:
        return place
    fast = count // 4
    inner = lax.min(place, 1) * lax.min(lax.max(4 * (fast - 1) + 1 - place, 0), 1)
    along = lax.max(place - 1, 0)
    row, step = lax.div(along, fast - 1), lax.rem(along, fast - 1)
    odd = lax.rem(row, 2)
    column = 1 + (1 - odd) * step + odd * (fast - 2 - step)
    return inner * (row * fast + column) + (1 - inner) * lax.rem(count - place, count) * fast


def ring_place(device, count):
    if count % 4 or count < 8:
        return device
    fast = count // 4
    row, column = lax.div(device, fast), lax.rem(device, fast)
    inner = lax.min(column, 1)
    odd = lax.rem(row, 2)
    within = 1 + row * (fast - 1) + (1 - odd) * (column - 1) + odd * (fast - 1 - column)
    return inner * within + (1 - inner) * lax.rem(count - row, count)


def gather_kernel(
    count, value_shard, output_shard, prior, value_all, output_all, work, strip,
    send, receive, own,
):
    me = lax.axis_index("dp")
    place = ring_place(me, count)
    targets = [
        ring_device(lax.rem(place + 1, count), count),
        ring_device(lax.rem(place + count - 1, count), count),
    ]
    shards, wholes = (value_shard, output_shard), (value_all, output_all)
    rows = value_shard.shape[0]
    half = rows // 2

    def piece(way, array, step, first):
        back = count - step if way == 0 else step
        origin = ring_device(lax.rem(place + back, count), count)
        start = pl.multiple_of(origin * rows + way * half, half)
        there = wholes[array].at[pl.ds(start, half), :]
        here = shards[array].at[pl.ds(way * half, half), :] if first else there
        return pltpu.make_async_remote_copy(
            src_ref=here,
            dst_ref=there,
            send_sem=send.at[way, array, step],
            recv_sem=receive.at[way, array, step],
            device_id={"dp": targets[way]},
            device_id_type=pl.DeviceIdType.MESH,
        )

    barrier = pltpu.get_barrier_semaphore()
    for target in targets:
        pl.semaphore_signal(
            barrier, inc=1, device_id={"dp": target}, device_id_type=pl.DeviceIdType.MESH
        )
    pl.semaphore_wait(barrier, 2)
    for array in range(2):
        for way in range(2):
            piece(way, array, 0, True).start()
    mine = pl.ds(pl.multiple_of(me * rows, rows), rows)
    kept = [
        pltpu.make_async_copy(shards[array], wholes[array].at[mine, :], own.at[array])
        for array in range(2)
    ]
    for copy in kept:
        copy.start()
    work[...] = prior[...]
    block = strip.shape[0]
    blocks = work.shape[0] // block

    def pass_on(array, step):
        for way in range(2):
            piece(way, array, step, False).wait_recv()

            @pl.when(step < count - 2)
            def _():
                piece(way, array, lax.min(step + 1, count - 2), False).start()

    @pl.loop(0, max(blocks, count - 1))
    def _(step):
        @pl.when(step < blocks)
        def _():
            sweep_strip(work, strip, step, block)

        @pl.when(step < count - 1)
        def _():
            pass_on(0, step)

        @pl.when(step < blocks)
        def _():
            sweep_rest(work, strip, step, block)

        @pl.when(step < count - 1)
        def _():
            pass_on(1, step)

    for copy in kept:
        copy.wait()
    for array in range(2):
        for way in range(2):
            piece(way, array, 0, True).wait_send()

            @pl.loop(1, count - 1)
            def _(step):
                piece(way, array, step, False).wait_send()


def gathered(value_shard, output_shard, prior):
    count = lax.axis_size("dp")
    rows, columns = value_shard.shape
    size = prior.shape[0]
    whole = jax.ShapeDtypeStruct((count * rows, columns), jnp.bfloat16)
    return pl.pallas_call(
        functools.partial(gather_kernel, count),
        out_shape=(whole, whole, jax.ShapeDtypeStruct((size, size), jnp.float32)),
        in_specs=[pl.BlockSpec(memory_space=pltpu.VMEM)] * 3,
        out_specs=(
            pl.BlockSpec(memory_space=pl.ANY),
            pl.BlockSpec(memory_space=pl.ANY),
            pl.BlockSpec(memory_space=pltpu.VMEM),
        ),
        scratch_shapes=[
            pltpu.VMEM((128, size), jnp.float32),
            pltpu.SemaphoreType.DMA((2, 2, count - 1)),
            pltpu.SemaphoreType.DMA((2, 2, count - 1)),
            pltpu.SemaphoreType.DMA((2,)),
        ],
        compiler_params=pltpu.CompilerParams(
            collective_id=2, has_side_effects=True, vmem_limit_bytes=48 * 2**20
        ),
        name="gather_and_invert",
    )(value_shard, output_shard, prior)


def score_kernel(everyone, negated, queries, out):
    grads = everyone[...]
    half = jnp.dot(grads, negated[...], precision=HIGHEST, preferred_element_type=jnp.float32)
    gram = -lax.dot_general(
        half, grads, (((1,), (1,)), ((), ())), precision=HIGHEST,
        preferred_element_type=jnp.float32,
    )
    count = grads.shape[0]
    rows = lax.broadcasted_iota(jnp.int32, (count, count), 0)
    columns = lax.broadcasted_iota(jnp.int32, (count, count), 1)
    inverse = inverted(gram + jnp.where(rows == columns, 1.0, 0.0))
    full = jnp.dot(gram, inverse, precision=HIGHEST, preferred_element_type=jnp.float32)
    owners = lax.broadcasted_iota(jnp.int32, (count, queries.shape[1]), 0)
    selector = jnp.where(owners == queries[...], 1.0, 0.0)
    out[...] = jnp.dot(full, selector, precision=HIGHEST, preferred_element_type=jnp.float32)


def all_scores(everyone, negated, queries):
    return pl.pallas_call(
        score_kernel,
        out_shape=jax.ShapeDtypeStruct((everyone.shape[0], queries.shape[0]), jnp.float32),
        in_specs=[pl.BlockSpec(memory_space=pltpu.VMEM)] * 3,
        out_specs=pl.BlockSpec(memory_space=pltpu.VMEM),
        compiler_params=pltpu.CompilerParams(vmem_limit_bytes=24 * 2**20),
        name="all_scores",
    )(everyone, negated, queries[None, :])


MESH = pl.DeviceIdType.MESH
CONTRACT_LAST = (((1,), (1,)), ((), ()))


def relay_kernel(
    sections, batches, example_rows,
    inputs, targets, gain, value_map, output_map, input_map, output_map_small,
    grads,
    hidden, following, cotangent, previous, values, normed, activated, features, factors,
    forward_send, forward_receive, backward_send, backward_receive,
):
    me = lax.axis_index("section")
    has_before, has_after = me > 0, me < sections - 1
    before, after = lax.max(me - 1, 0), lax.min(me + 1, sections - 1)
    width, value_width = value_map.shape
    signal_width = output_map_small.shape[0]
    chunks = forward_send.shape[1]
    chunk = width // chunks
    tile = 256
    group = 16

    def span(index, size):
        return pl.ds(pl.multiple_of(index * size, size), size)

    def forward_copy(batch, piece):
        columns = span(piece, chunk)
        return pltpu.make_async_remote_copy(
            src_ref=following.at[batch, :, columns],
            dst_ref=hidden.at[batch, :, columns],
            send_sem=forward_send.at[batch, piece],
            recv_sem=forward_receive.at[batch, piece],
            device_id={"section": after},
            device_id_type=MESH,
        )

    def backward_copy(batch, piece):
        columns = span(piece, chunk)
        return pltpu.make_async_remote_copy(
            src_ref=previous.at[batch, :, columns],
            dst_ref=cotangent.at[batch, :, columns],
            send_sem=backward_send.at[batch, piece],
            recv_sem=backward_receive.at[batch, piece],
            device_id={"section": before},
            device_id_type=MESH,
        )

    barrier = pltpu.get_barrier_semaphore()

    @pl.when(has_before)
    def _():
        pl.semaphore_signal(barrier, inc=1, device_id={"section": before}, device_id_type=MESH)

    @pl.when(has_after)
    def _():
        pl.semaphore_signal(barrier, inc=1, device_id={"section": after}, device_id_type=MESH)

    peers = lax.min(me, 1) + lax.min(sections - 1 - me, 1)
    pl.semaphore_wait(barrier, peers)

    @pl.loop(0, batches)
    def _(batch):
        @pl.when(has_before)
        def _():
            @pl.loop(0, chunks)
            def _(piece):
                forward_copy(batch, piece).wait_recv()

        @pl.when(jnp.logical_not(has_before))
        def _():
            hidden[batch] = inputs[batch]

        @pl.loop(0, example_rows // group)
        def _(at):
            rows = span(at, group)
            widened = hidden[batch, rows, :].astype(jnp.float32)
            factor = lax.rsqrt(jnp.mean(widened * widened, axis=-1, keepdims=True) + 1e-05)
            factors[batch, rows, :] = factor
            normed[rows, :] = (widened * factor * gain[...]).astype(jnp.bfloat16)

        @pl.loop(0, value_width // tile)
        def _(at):
            columns = span(at, tile)
            found = jnp.dot(
                normed[...], value_map[:, columns], preferred_element_type=jnp.float32
            )
            values[batch, :, columns] = found
            activated[:, columns] = (found / (1.0 + jnp.exp(-found))).astype(jnp.bfloat16)

        @pl.when(has_after)
        def _():
            @pl.loop(0, chunks)
            def _(piece):
                columns = span(piece, chunk)
                branch = lax.dot_general(
                    activated[...], output_map[columns, :], CONTRACT_LAST,
                    preferred_element_type=jnp.float32,
                )
                following[batch, :, columns] = (
                    hidden[batch, :, columns].astype(jnp.float32) + branch
                ).astype(jnp.bfloat16)
                forward_copy(batch, piece).start()

        features[batch] = lax.dot_general(
            normed[...], input_map[...], CONTRACT_LAST, preferred_element_type=jnp.float32
        ).astype(jnp.bfloat16)

    @pl.loop(0, batches)
    def _(batch):
        @pl.when(has_after)
        def _():
            @pl.loop(0, chunks)
            def _(piece):
                backward_copy(batch, piece).wait_recv()

        @pl.when(jnp.logical_not(has_after))
        def _():
            cotangent[batch] = targets[batch]

        slopes = activated

        def upstream_tile(at, total):
            columns = span(at, tile)
            upstream = jnp.dot(
                cotangent[batch], output_map[:, columns], preferred_element_type=jnp.float32
            )
            found = values[batch, :, columns]
            logistic = 1.0 / (1.0 + jnp.exp(-found))
            slope = (upstream * logistic * (1.0 + found * (1.0 - logistic))).astype(jnp.bfloat16)
            slopes[:, columns] = slope
            return total + jnp.sum(slope.astype(jnp.float32) * found, axis=-1, keepdims=True)

        total = lax.fori_loop(
            0, value_width // tile, upstream_tile, jnp.zeros((example_rows, 1), jnp.float32)
        )
        factor = factors[batch]
        shrink = total * (factor * factor) * (1.0 / width)

        @pl.when(has_before)
        def _():
            @pl.loop(0, chunks)
            def _(piece):
                columns = span(piece, chunk)
                normed_grad = lax.dot_general(
                    slopes[...], value_map[columns, :], CONTRACT_LAST,
                    preferred_element_type=jnp.float32,
                )
                weighted = normed_grad * gain[:, columns]
                hidden_grad = (
                    factor * weighted - hidden[batch, :, columns].astype(jnp.float32) * shrink
                )
                previous[batch, :, columns] = (
                    cotangent[batch, :, columns].astype(jnp.float32) + hidden_grad
                ).astype(jnp.bfloat16)
                backward_copy(batch, piece).start()

        signals = lax.dot_general(
            slopes[...], output_map_small[...], CONTRACT_LAST, preferred_element_type=jnp.float32
        ).astype(jnp.bfloat16)
        grads[batch] = lax.dot_general(
            signals, features[batch], (((0,), (0,)), ((), ())), preferred_element_type=jnp.float32
        ) * (1.0 / example_rows)

    @pl.loop(0, batches)
    def _(batch):
        @pl.loop(0, chunks)
        def _(piece):
            @pl.when(has_after)
            def _():
                forward_copy(batch, piece).wait_send()

            @pl.when(has_before)
            def _():
                backward_copy(batch, piece).wait_send()


def relay(inputs, targets, gain, value_map, output_map, input_map, output_map_small):
    batches, example_rows, width = inputs.shape
    value_width = value_map.shape[1]
    feature_width = input_map.shape[0]
    signal_width = output_map_small.shape[0]
    chunks = 8
    stream = pltpu.VMEM((batches, example_rows, width), jnp.bfloat16)
    return pl.pallas_call(
        functools.partial(relay_kernel, lax.axis_size("section"), batches, example_rows),
        out_shape=jax.ShapeDtypeStruct((batches, signal_width, feature_width), jnp.float32),
        in_specs=[pl.BlockSpec(memory_space=pltpu.VMEM)] * 7,
        out_specs=pl.BlockSpec(memory_space=pltpu.VMEM),
        scratch_shapes=[
            stream, stream, stream, stream,
            pltpu.VMEM((batches, example_rows, value_width), jnp.float32),
            pltpu.VMEM((example_rows, width), jnp.bfloat16),
            pltpu.VMEM((example_rows, value_width), jnp.bfloat16),
            pltpu.VMEM((batches, example_rows, feature_width), jnp.bfloat16),
            pltpu.VMEM((batches, example_rows, 1), jnp.float32),
        ] + [pltpu.SemaphoreType.DMA((batches, chunks))] * 4,
        compiler_params=pltpu.CompilerParams(
            collective_id=1, has_side_effects=True, vmem_limit_bytes=48 * 2**20
        ),
        name="relay",
    )(inputs, targets, gain, value_map, output_map, input_map, output_map_small)


def per_device(
    inputs,
    output_cotangent,
    lengths,
    query_examples,
    norm_gain,
    value_weight,
    output_weight,
    input_projection,
    output_projection,
    fisher_prior,
):
    value_map, output_map, negated_inverse = gathered(
        value_weight[0], output_weight[0], fisher_prior[0]
    )
    gain = norm_gain.astype(jnp.float32)
    input_map = input_projection[0]
    output_map_small = output_projection[0]
    batches = lengths.shape[0]
    example_rows = inputs.shape[0] // batches
    width = inputs.shape[1]
    feature_width = input_map.shape[0]
    signal_width = output_map_small.shape[0]
    entries = inputs.reshape(batches, example_rows, width)
    positions = jnp.arange(example_rows, dtype=jnp.int32)
    keep = (positions[None, :] < lengths[:, None]).astype(jnp.bfloat16)
    targets = output_cotangent.reshape(batches, example_rows, width) * keep[:, :, None]
    saved_grads = relay(
        entries, targets, gain, value_map, output_map, input_map, output_map_small
    )
    flat = saved_grads.reshape(batches, signal_width * feature_width)
    everyone = lax.all_gather(flat, "dp", axis=0, tiled=True)
    every_score = all_scores(everyone, negated_inverse, query_examples)
    section_scores = lax.dynamic_slice_in_dim(
        every_score, lax.axis_index("dp") * batches, batches, 0
    )
    return lax.psum(section_scores, "section")


def solution(mesh):
    placed = (
        P("dp", None),
        P("dp", None),
        P("dp"),
        P(),
        P("section", None),
        P("section", "dp", None),
        P("section", "dp", None),
        P("section", None, None),
        P("section", None, None),
        P("section", None, None),
    )
    return jax.shard_map(
        per_device, mesh=mesh, in_specs=placed, out_specs=P("dp", None), check_vma=False
    )
```

profile of v0, /device:TPU:0, one launch (start us, length us, event | category | flops | bytes accessed | tf_op | source)
XLA Modules:
  0.0 322.5 jit_solution(9971630644567203761)
XLA Ops:
  0.0 0.0 copy-start.2
  0.0 1.2 copy-done.2
  1.2 0.0 copy-start.3
  1.2 1.2 copy-done.3
  2.5 0.0 copy-start.9
  2.5 0.0 copy-start.7
  2.5 188.4 %gather_and_invert.1 = (bf16[4096,1024]{1,0:T(8,128)(2,1)}, bf16[4096,1024]{1,0:T(8,128)(2,1)}, f32[1024,1024]{1,0:T(8,128)}) custom-call(bf16[512,1024]{1,0:T(8,128)(2,1)S(1)} %bitcast.9, bf16[512,1024]{1,0:T(8,128)(2,1)S(1)} %bitcast.10, f32[1024,1024]{1,0:T(8,128)} %bitcast.14), custom_call_target="tpu_custom_call" | custom-call | tf_op jit(solution)/shard_map/gather_and_invert/pallas_call | solution.py:175
  190.8 0.0 copy-done.9
  190.8 0.1 compare_convert_fusion
  190.9 0.0 copy-done.7
  190.9 0.0 copy-start.8
  190.9 0.0 copy-start.1
  190.9 0.0 copy-start.4
  190.9 0.0 copy-start.5
  190.9 0.2 broadcast_multiply_fusion.targets
  191.1 0.5 copy-done.8
  191.7 0.7 copy-done.1
  192.3 0.0 copy-done.4
  192.4 0.0 copy-done.5
  192.4 0.0 copy-start.6
  192.4 87.0 %relay.1 = f32[2,32,32]{2,1,0:T(8,128)S(1)} custom-call(bf16[2,96,4096]{2,1,0:T(8,128)(2,1)S(1)} %bitcast.8, bf16[2,96,4096]{2,1,0:T(8,128)(2,1)S(1)} %broadcast_multiply_fusion.targets, f32[1,4096]{1,0:T(1,128)S(1)} %convert_element_type.11.gain, bf16[4096,1024]{1,0:T(8,128)(2,1)} %get-tuple-element.8.value_map, ...), custom_call_target="tpu_custom_call" | custom-call | tf_op jit(solution)/shard_map/relay/pallas_call | solution.py:407
  279.4 0.1 reshape.34
  279.5 30.5 %all-gather = f32[8,2,1024]{2,1,0:T(2,128)S(1)} all-gather(f32[1,2,1024]{2,1,0:T(2,128)S(1)} %reshape.34), channel_id=1, replica_groups=mesh['section'=4,'dp'=8] {'dp'}, dimensions={0}, use_global_device_ids=true | all-gather | bytes 73728 | tf_op jit(solution)/shard_map/all_gather | solution.py:458
  310.1 0.0 copy-done.6
  310.1 0.0 copy-start
  310.1 2.2 copy-done
  312.3 3.9 %all_scores.1 = f32[16,16]{1,0:T(8,128)S(1)} custom-call(f32[16,1024]{1,0:T(8,128)S(1)} %reshape.35.everyone, f32[1024,1024]{1,0:T(8,128)S(1)} %copy-done, s32[1,16]{1,0:T(1,128)S(1)} %bitcast.13), custom_call_target="tpu_custom_call" | custom-call | tf_op jit(solution)/shard_map/all_scores/pallas_call | solution.py:215
  316.2 6.3 %psum.7 = f32[2,16]{1,0:T(2,128)} all-reduce(f32[2,16]{1,0:T(2,128)S(1)} %constant_dynamic-slice_fusion), channel_id=1, replica_groups=mesh['section'=4,'dp'=8] {'section'}, use_global_device_ids=true, to_apply=%region_0.0 | all-reduce | flops 32 | bytes 256 | tf_op jit(solution)/shard_map/psum | solution.py:463
  (3 shorter events, 0.1 us)
Async XLA Ops:
  0.0 1.2 copy-start.2
  1.2 1.2 copy-start.3
  2.5 188.4 %copy-start.9 = (s32[2]{0:T(128)S(1)}, s32[2]{0:T(128)}, u32[]{:S(2)}) copy-start(s32[2]{0:T(128)} %param.12) | copy-start | bytes 28
  2.5 188.5 %copy-start.7 = (bf16[192,4096]{1,0:T(8,128)(2,1)S(1)}, bf16[192,4096]{1,0:T(8,128)(2,1)}, u32[]{:S(2)}) copy-start(bf16[192,4096]{1,0:T(8,128)(2,1)} %param.11) | copy-start | bytes 4718596
  190.9 0.7 copy-start.8
  190.9 1.4 copy-start.1
  190.9 1.4 copy-start.4
  190.9 1.4 copy-start.5
  192.4 117.7 %copy-start.6 = (s32[16]{0:T(128)S(1)}, s32[16]{0:T(128)}, u32[]{:S(2)}) copy-start(s32[16]{0:T(128)} %param.13) | copy-start | bytes 196
  310.1 2.2 copy-start
where the time goes:
time: 323 us
  Pallas kernels  279 us (86%)
  blocking collectives  36.8 us (11%)
  local copies, waits for them, and re-layouts  6.01 us (2%)
    pallas_call x1, Pallas kernels, gathered(): pl.pallas_call(functools.partial(gather_kernel, count), out_shape=(whole,...  188 us
    pallas_call x1, Pallas kernels, relay(): pl.pallas_call(functools.partial(relay_kernel, lax.axis_size('section'),...  87 us
    all_gather x1, blocking collectives, per_device(): everyone = lax.all_gather(flat, 'dp', axis=0, tiled=True)  30.5 us

commit v1 on v0

v1 whole, which is shorter than its diff:
```python
import functools

import jax
import jax.numpy as jnp
from jax import lax
from jax.experimental import pallas as pl
from jax.experimental.pallas import tpu as pltpu
from jax.sharding import PartitionSpec as P


HIGHEST = lax.Precision.HIGHEST


def inverted(block):
    size = block.shape[0]
    rows = lax.broadcasted_iota(jnp.int32, block.shape, 0)
    columns = lax.broadcasted_iota(jnp.int32, block.shape, 1)

    def sweep(pivot, held):
        at_row, at_column = rows == pivot, columns == pivot
        row = jnp.sum(jnp.where(at_row, held, 0.0), axis=0, keepdims=True)
        column = jnp.sum(jnp.where(at_column, held, 0.0), axis=1, keepdims=True)
        corner = jnp.sum(jnp.where(at_column[:1], row, 0.0), axis=1, keepdims=True)
        scale = 1.0 / corner
        scaled = row * scale
        updated = held - column * scaled
        updated = jnp.where(at_row, scaled, updated)
        updated = jnp.where(at_column, column * scale, updated)
        return jnp.where(at_row & at_column, -scale, updated)

    return -lax.fori_loop(0, size, sweep, block)


def sweep_strip(work, strip, step, block):
    span = pl.ds(pl.multiple_of(step * block, block), block)
    corner = inverted(work[span, span])
    strip[...] = jnp.dot(
        corner, work[span, :], precision=HIGHEST, preferred_element_type=jnp.float32
    )
    strip[:, span] = -corner


def sweep_rest(work, strip, step, block):
    span = pl.ds(pl.multiple_of(step * block, block), block)

    @pl.loop(0, work.shape[0] // block)
    def _(other):
        across = pl.ds(pl.multiple_of(other * block, block), block)

        @pl.when(other != step)
        def _():
            work[across, :] -= jnp.dot(
                work[span, across].T, strip[...], precision=HIGHEST,
                preferred_element_type=jnp.float32,
            )
            work[across, span] = strip[:, across].T

    work[span, :] = strip[...]


MESH = pl.DeviceIdType.MESH
CONTRACT_LAST = (((1,), (1,)), ((), ()))
PAIR = 2
PIECES = 4
BLOCK = 128
LANES = 128


def flipped(device, bit):
    return device + (1 - 2 * lax.rem(lax.div(device, bit), 2)) * bit


def mate(device, mask):
    bit = 1
    while bit <= mask:
        if mask & bit:
            device = flipped(device, bit)
        bit *= 2
    return device


def slot_of(device):
    return lax.div(device, 2 * PAIR) * PAIR + lax.rem(device, PAIR)


def gather_events(count):
    bits = []
    bit = count // 2
    while bit >= 1:
        if bit != PAIR:
            bits.append(bit)
        bit //= 2
    held, events = [0], []
    for bit in bits:
        events += [(bit, mask) for mask in held]
        held += [mask | bit for mask in held]
    return events


def span(index, size):
    return pl.ds(pl.multiple_of(index * size, size), size)


def window_kernel(
    sections, count,
    inputs, targets, gain, value_shard, output_shard, input_map, output_map_small, prior, queries,
    scores,
    weights, work, strip, hidden, following, cotangent, previous, values, upstream, normed,
    activated, features, factors, squares, gain_half, input_half, first_out, first_in,
    extra_out, extra_in, second_out, second_in, flats, everyone, rows_all, final,
    gather_send, gather_receive, own_weights, prior_done, entry_own, entry_send, entry_receive,
    forward_send, forward_receive, backward_send, backward_receive,
    first_send, first_receive, extra_send, extra_receive, second_send, second_receive,
    publish_send, publish_receive, final_send, final_receive,
):
    section, me = lax.axis_index("section"), lax.axis_index("dp")
    has_before, has_after = section > 0, section < sections - 1
    before, after = lax.max(section - 1, 0), lax.min(section + 1, sections - 1)
    side = lax.rem(lax.div(me, PAIR), 2)
    partner = flipped(me, PAIR)
    batches, length, width = inputs.shape
    entries = 2 * batches
    half, value_width = weights.shape[1], weights.shape[2]
    rows = value_shard.shape[0]
    piece_rows = rows // PIECES
    stretch = PAIR * rows
    stretches = half // stretch
    size = work.shape[0]
    blocks = size // BLOCK
    feature_width = input_map.shape[0]
    signal_width = output_map_small.shape[0]
    chunks = forward_send.shape[1]
    chunk = half // chunks
    tiles = first_send.shape[1]
    tile = value_width // tiles
    group = 16
    shards = (value_shard, output_shard)
    value_map, output_map = weights.at[0], weights.at[1]
    events = gather_events(count)

    def gather_copy(number, array, piece, first):
        bit, mask = events[number]
        at = slot_of(mate(me, mask)) * PIECES + piece
        there = weights.at[array, span(at, piece_rows), :]
        here = shards[array].at[span(piece, piece_rows), :] if first else there
        return pltpu.make_async_remote_copy(
            src_ref=here,
            dst_ref=there,
            send_sem=gather_send.at[number, array, piece],
            recv_sem=gather_receive.at[number, array, piece],
            device_id={"dp": flipped(me, bit)},
            device_id_type=MESH,
        )

    def serve(array, piece):
        for number, (bit, mask) in enumerate(events):
            forwards = [later for later, (_, want) in enumerate(events) if want == bit | mask]
            if forwards:
                gather_copy(number, array, piece, False).wait_recv()
            for later in forwards:
                gather_copy(later, array, piece, False).start()

    def collect(array):
        for number, (bit, mask) in enumerate(events):
            if all(want != bit | mask for _, want in events):
                @pl.loop(0, PIECES)
                def _(piece):
                    gather_copy(number, array, piece, False).wait_recv()

        kept[array].wait()

    def entry_copy(kind, entry, part, remote):
        source = (inputs, targets)[kind]
        sink = (hidden, cotangent)[kind]
        wanted = 1 - side if remote else side
        here = source.at[entry, :, span(2 * part + wanted, stretch)]
        there = sink.at[side * batches + entry, :, span(part, stretch)]
        if not remote:
            return pltpu.make_async_copy(here, there, entry_own.at[kind, entry, part])
        return pltpu.make_async_remote_copy(
            src_ref=here,
            dst_ref=there,
            send_sem=entry_send.at[kind, entry, part],
            recv_sem=entry_receive.at[kind, entry, part],
            device_id={"dp": partner},
            device_id_type=MESH,
        )

    def entry_wait(kind, batch):
        sink = (hidden, cotangent)[kind]
        owner, entry = lax.div(batch, batches), lax.rem(batch, batches)
        for part in range(stretches):
            there = sink.at[batch, :, span(part, stretch)]

            @pl.when(owner == side)
            def _():
                pltpu.make_async_copy(there, there, entry_own.at[kind, entry, part]).wait()

            @pl.when(owner != side)
            def _():
                pltpu.make_async_remote_copy(
                    src_ref=there,
                    dst_ref=there,
                    send_sem=entry_send.at[kind, entry, part],
                    recv_sem=entry_receive.at[kind, entry, part],
                    device_id={"dp": partner},
                    device_id_type=MESH,
                ).wait_recv()

    def hop(source, sink, send, receive, device, batch, piece):
        columns = span(piece, chunk)
        return pltpu.make_async_remote_copy(
            src_ref=source.at[batch, :, columns],
            dst_ref=sink.at[batch, :, columns],
            send_sem=send.at[batch, piece],
            recv_sem=receive.at[batch, piece],
            device_id={"section": device},
            device_id_type=MESH,
        )

    def forward_copy(batch, piece):
        return hop(following, hidden, forward_send, forward_receive, after, batch, piece)

    def backward_copy(batch, piece):
        return hop(previous, cotangent, backward_send, backward_receive, before, batch, piece)

    def swap(source, sink, send, receive, batch, at):
        columns = span(at, tile)
        return pltpu.make_async_remote_copy(
            src_ref=source.at[batch, :, columns],
            dst_ref=sink.at[batch, :, columns],
            send_sem=send.at[batch, at],
            recv_sem=receive.at[batch, at],
            device_id={"dp": partner},
            device_id_type=MESH,
        )

    def first_copy(batch, at):
        return swap(first_out, first_in, first_send, first_receive, batch, at)

    def second_copy(batch, at):
        return swap(second_out, second_in, second_send, second_receive, batch, at)

    def extra_copy(batch):
        return pltpu.make_async_remote_copy(
            src_ref=extra_out.at[batch],
            dst_ref=extra_in.at[batch],
            send_sem=extra_send.at[batch],
            recv_sem=extra_receive.at[batch],
            device_id={"dp": partner},
            device_id_type=MESH,
        )

    def invert_step(step):
        sweep_strip(work, strip, step, BLOCK)
        sweep_rest(work, strip, step, BLOCK)

    prior_copy = pltpu.make_async_copy(prior, work, prior_done)
    prior_copy.start()
    mine = span(slot_of(me), rows)
    kept = [
        pltpu.make_async_copy(shards[array], weights.at[array, mine, :], own_weights.at[array])
        for array in range(2)
    ]
    barrier = pltpu.get_barrier_semaphore()

    @pl.loop(1, count)
    def _(offset):
        pl.semaphore_signal(
            barrier, inc=1, device_id={"dp": lax.rem(me + offset, count)}, device_id_type=MESH
        )

    @pl.loop(1, sections)
    def _(offset):
        pl.semaphore_signal(
            barrier, inc=1, device_id={"section": lax.rem(section + offset, sections)},
            device_id_type=MESH,
        )

    pl.semaphore_wait(barrier, count + sections - 2)

    for kind, wanted in ((0, jnp.logical_not(has_before)), (1, jnp.logical_not(has_after))):
        @pl.when(wanted)
        def _():
            for entry in range(batches):
                for part in range(stretches):
                    entry_copy(kind, entry, part, True).start()
                    entry_copy(kind, entry, part, False).start()

    for array in range(2):
        for piece in range(PIECES):
            for number, (_, mask) in enumerate(events):
                if mask == 0:
                    gather_copy(number, array, piece, True).start()
    for copy in kept:
        copy.start()

    input_half[...] = jnp.zeros_like(input_half)
    for part in range(stretches):
        there = pl.ds(part * stretch, stretch)
        here = span(2 * part + side, stretch)
        gain_half[:, there] = gain[:, here]
        input_half[:feature_width, there] = input_map[:, here]
    prior_copy.wait()

    early = min(blocks, PIECES)
    rest = blocks - early

    @pl.loop(0, PIECES)
    def _(step):
        @pl.when(step < early)
        def _():
            sweep_strip(work, strip, step, BLOCK)

        first = 2 * step
        serve(lax.div(first, PIECES), lax.rem(first, PIECES))

        @pl.when(step < early)
        def _():
            sweep_rest(work, strip, step, BLOCK)

        second = first + 1
        serve(lax.div(second, PIECES), lax.rem(second, PIECES))

    collect(0)
    edge = lax.div(rest * section, 2 * max(sections - 1, 1))

    @pl.loop(early, early + edge)
    def _(step):
        invert_step(step)

    @pl.loop(0, entries)
    def _(batch):
        @pl.when(has_before)
        def _():
            @pl.loop(0, chunks)
            def _(piece):
                forward_copy(batch, piece).wait_recv()

        @pl.when(jnp.logical_not(has_before))
        def _():
            entry_wait(0, batch)

        @pl.loop(0, length // group)
        def _(at):
            part = span(at, group)
            widened = hidden[batch, part, :].astype(jnp.float32)
            squares[part, :] = jnp.sum(widened * widened, axis=-1, keepdims=True)
            normed[part, :] = (widened * gain_half[...]).astype(jnp.bfloat16)

        extras = lax.dot_general(
            normed[...], input_half[...], CONTRACT_LAST, preferred_element_type=jnp.float32
        )
        lanes = lax.broadcasted_iota(jnp.int32, extras.shape, 1)
        extra_out[batch] = jnp.where(lanes == feature_width, squares[...], extras)
        extra_copy(batch).start()

        @pl.loop(0, tiles)
        def _(at):
            columns = span(at, tile)
            found = jnp.dot(
                normed[...], value_map[:, columns], preferred_element_type=jnp.float32
            )
            values[batch, :, columns] = found
            first_out[batch, :, columns] = found.astype(jnp.bfloat16)
            first_copy(batch, at).start()

        extra_copy(batch).wait_recv()
        both = extra_out[batch] + extra_in[batch]
        total = both[:, feature_width : feature_width + 1]
        factor = lax.rsqrt(total * (1.0 / width) + 1e-05)
        factors[batch] = factor
        features[batch] = (both[:, :feature_width] * factor).astype(jnp.bfloat16)

        @pl.loop(0, tiles)
        def _(at):
            columns = span(at, tile)
            first_copy(batch, at).wait_recv()
            partial = first_in[batch, :, columns].astype(jnp.float32)
            found = (values[batch, :, columns] + partial) * factors[batch]
            values[batch, :, columns] = found
            activated[:, columns] = (found / (1.0 + jnp.exp(-found))).astype(jnp.bfloat16)

        @pl.when(batch == 0)
        def _():
            collect(1)

        @pl.when(has_after)
        def _():
            @pl.loop(0, chunks)
            def _(piece):
                columns = span(piece, chunk)
                branch = lax.dot_general(
                    activated[...], output_map[columns, :], CONTRACT_LAST,
                    preferred_element_type=jnp.float32,
                )
                following[batch, :, columns] = (
                    hidden[batch, :, columns].astype(jnp.float32) + branch
                ).astype(jnp.bfloat16)
                forward_copy(batch, piece).start()

    @pl.loop(early + edge, blocks - edge)
    def _(step):
        invert_step(step)

    @pl.loop(0, entries)
    def _(batch):
        @pl.when(has_after)
        def _():
            @pl.loop(0, chunks)
            def _(piece):
                backward_copy(batch, piece).wait_recv()

        @pl.when(jnp.logical_not(has_after))
        def _():
            entry_wait(1, batch)

        @pl.loop(0, tiles)
        def _(at):
            columns = span(at, tile)
            found = jnp.dot(
                cotangent[batch], output_map[:, columns], preferred_element_type=jnp.float32
            )
            upstream[:, columns] = found
            second_out[batch, :, columns] = found.astype(jnp.bfloat16)
            second_copy(batch, at).start()

        slopes = activated

        def slope_tile(at, total):
            columns = span(at, tile)
            second_copy(batch, at).wait_recv()
            arrived = upstream[:, columns] + second_in[batch, :, columns].astype(jnp.float32)
            found = values[batch, :, columns]
            logistic = 1.0 / (1.0 + jnp.exp(-found))
            slope = (arrived * logistic * (1.0 + found * (1.0 - logistic))).astype(jnp.bfloat16)
            slopes[:, columns] = slope
            return total + jnp.sum(slope.astype(jnp.float32) * found, axis=-1, keepdims=True)

        total = lax.fori_loop(0, tiles, slope_tile, jnp.zeros((length, 1), jnp.float32))
        factor = factors[batch]
        shrink = total * (factor * factor) * (1.0 / width)

        @pl.when(has_before)
        def _():
            @pl.loop(0, chunks)
            def _(piece):
                columns = span(piece, chunk)
                normed_grad = lax.dot_general(
                    slopes[...], value_map[columns, :], CONTRACT_LAST,
                    preferred_element_type=jnp.float32,
                )
                weighted = normed_grad * gain_half[:, columns]
                hidden_grad = (
                    factor * weighted - hidden[batch, :, columns].astype(jnp.float32) * shrink
                )
                previous[batch, :, columns] = (
                    cotangent[batch, :, columns].astype(jnp.float32) + hidden_grad
                ).astype(jnp.bfloat16)
                backward_copy(batch, piece).start()

        signals = lax.dot_general(
            slopes[...], output_map_small[...], CONTRACT_LAST, preferred_element_type=jnp.float32
        ).astype(jnp.bfloat16)
        shape = (signal_width, size)
        entry = lax.broadcasted_iota(jnp.int32, shape, 1)
        line = lax.broadcasted_iota(jnp.int32, shape, 0)
        outer = jnp.where(lax.div(entry, feature_width) == line, 1.0, 0.0).astype(jnp.bfloat16)
        shape = (feature_width, size)
        entry = lax.broadcasted_iota(jnp.int32, shape, 1)
        line = lax.broadcasted_iota(jnp.int32, shape, 0)
        inner = jnp.where(lax.rem(entry, feature_width) == line, 1.0, 0.0).astype(jnp.bfloat16)
        left = jnp.dot(signals, outer, preferred_element_type=jnp.float32)
        right = jnp.dot(features[batch], inner, preferred_element_type=jnp.float32)
        flat = jnp.sum(left * right, axis=0, keepdims=True) * (1.0 / length)
        flats[lax.div(batch, batches), pl.ds(lax.rem(batch, batches), 1), :] = flat

    @pl.loop(blocks - edge, blocks)
    def _(step):
        invert_step(step)

    everyone[me] = flats[side]

    def publish(offset, origin):
        return pltpu.make_async_remote_copy(
            src_ref=everyone.at[origin],
            dst_ref=everyone.at[origin],
            send_sem=publish_send.at[offset],
            recv_sem=publish_receive.at[offset],
            device_id={"dp": lax.rem(me + offset, count)},
            device_id_type=MESH,
        )

    @pl.loop(1, count)
    def _(offset):
        publish(offset, me).start()

    @pl.loop(1, count)
    def _(offset):
        publish(offset, lax.rem(me + count - offset, count)).wait_recv()

    for device in range(count):
        rows_all[device * batches : (device + 1) * batches, :] = everyone[device]
    grads = rows_all[...]
    examples = count * batches
    product = jnp.dot(grads, work[...], precision=HIGHEST, preferred_element_type=jnp.float32)
    gram = -lax.dot_general(
        product, grads, CONTRACT_LAST, precision=HIGHEST, preferred_element_type=jnp.float32
    )
    shape = (examples, examples)
    diagonal = lax.broadcasted_iota(jnp.int32, shape, 0) == lax.broadcasted_iota(jnp.int32, shape, 1)
    inverse = inverted(gram + jnp.where(diagonal, 1.0, 0.0))
    picked = lax.broadcasted_iota(jnp.int32, (8, examples), 0)
    columns = lax.broadcasted_iota(jnp.int32, (8, examples), 1)
    pick = jnp.where((columns == me * batches + picked) & (picked < batches), 1.0, 0.0)
    owners = lax.broadcasted_iota(jnp.int32, (examples, queries.shape[1]), 0)
    selector = jnp.where(owners == queries[...], 1.0, 0.0)
    ours = jnp.dot(pick, gram, precision=HIGHEST, preferred_element_type=jnp.float32)
    chosen = jnp.dot(inverse, selector, precision=HIGHEST, preferred_element_type=jnp.float32)
    final[section] = jnp.dot(ours, chosen, precision=HIGHEST, preferred_element_type=jnp.float32)

    def finish(offset, origin):
        return pltpu.make_async_remote_copy(
            src_ref=final.at[origin],
            dst_ref=final.at[origin],
            send_sem=final_send.at[offset],
            recv_sem=final_receive.at[offset],
            device_id={"section": lax.rem(section + offset, sections)},
            device_id_type=MESH,
        )

    @pl.loop(1, sections)
    def _(offset):
        finish(offset, section).start()

    @pl.loop(1, sections)
    def _(offset):
        finish(offset, lax.rem(section + sections - offset, sections)).wait_recv()

    result = final[0]
    for other in range(1, sections):
        result = result + final[other]
    scores[...] = result[: scores.shape[0], : scores.shape[1]]

    @pl.loop(1, sections)
    def _(offset):
        finish(offset, section).wait_send()

    @pl.loop(1, count)
    def _(offset):
        publish(offset, me).wait_send()

    for kind, wanted in ((0, jnp.logical_not(has_before)), (1, jnp.logical_not(has_after))):
        @pl.when(wanted)
        def _():
            for entry in range(batches):
                for part in range(stretches):
                    entry_copy(kind, entry, part, True).wait_send()

    for number, (_, mask) in enumerate(events):
        for array in range(2):
            @pl.loop(0, PIECES)
            def _(piece):
                gather_copy(number, array, piece, mask == 0).wait_send()

    @pl.loop(0, entries)
    def _(batch):
        extra_copy(batch).wait_send()

        @pl.loop(0, tiles)
        def _(at):
            first_copy(batch, at).wait_send()
            second_copy(batch, at).wait_send()

        @pl.loop(0, chunks)
        def _(piece):
            @pl.when(has_after)
            def _():
                forward_copy(batch, piece).wait_send()

            @pl.when(has_before)
            def _():
                backward_copy(batch, piece).wait_send()


def window(
    inputs, targets, gain, value_shard, output_shard, input_map, output_map_small, prior, queries
):
    sections, count = lax.axis_size("section"), lax.axis_size("dp")
    batches, length, width = inputs.shape
    rows, value_width = value_shard.shape
    entries = 2 * batches
    half = width // 2
    size = prior.shape[0]
    feature_width = input_map.shape[0]
    asked = queries.shape[0]
    padded = jnp.full((1, LANES * pl.cdiv(asked, LANES)), -1, jnp.int32)
    padded = lax.dynamic_update_slice(padded, queries[None, :], (0, 0))
    chunks, tiles = 8, 4
    events = len(gather_events(count))
    stretches = half // (PAIR * rows)
    dma = pltpu.SemaphoreType.DMA
    stream = pltpu.VMEM((entries, length, half), jnp.bfloat16)
    parts = pltpu.VMEM((entries, length, value_width), jnp.bfloat16)
    extra = pltpu.VMEM((entries, length, LANES), jnp.float32)
    anywhere = pl.BlockSpec(memory_space=pl.ANY)
    inside = pl.BlockSpec(memory_space=pltpu.VMEM)
    return pl.pallas_call(
        functools.partial(window_kernel, sections, count),
        out_shape=jax.ShapeDtypeStruct((batches, asked), jnp.float32),
        in_specs=[
            anywhere, anywhere, inside, anywhere, anywhere, inside, inside, anywhere, inside
        ],
        out_specs=inside,
        scratch_shapes=[
            pltpu.VMEM((2, half, value_width), jnp.bfloat16),
            pltpu.VMEM((size, size), jnp.float32),
            pltpu.VMEM((BLOCK, size), jnp.float32),
            stream, stream, stream, stream,
            pltpu.VMEM((entries, length, value_width), jnp.float32),
            pltpu.VMEM((length, value_width), jnp.float32),
            pltpu.VMEM((length, half), jnp.bfloat16),
            pltpu.VMEM((length, value_width), jnp.bfloat16),
            pltpu.VMEM((entries, length, feature_width), jnp.bfloat16),
            pltpu.VMEM((entries, length, 1), jnp.float32),
            pltpu.VMEM((length, 1), jnp.float32),
            pltpu.VMEM((1, half), jnp.float32),
            pltpu.VMEM((LANES, half), jnp.bfloat16),
            parts, parts, extra, extra, parts, parts,
            pltpu.VMEM((2, batches, size), jnp.float32),
            pltpu.VMEM((count, batches, size), jnp.float32),
            pltpu.VMEM((count * batches, size), jnp.float32),
            pltpu.VMEM((sections, 8, padded.shape[1]), jnp.float32),
            dma((events, 2, PIECES)), dma((events, 2, PIECES)), dma((2,)), dma,
            dma((2, batches, stretches)), dma((2, batches, stretches)),
            dma((2, batches, stretches)),
            dma((entries, chunks)), dma((entries, chunks)),
            dma((entries, chunks)), dma((entries, chunks)),
            dma((entries, tiles)), dma((entries, tiles)), dma((entries,)), dma((entries,)),
            dma((entries, tiles)), dma((entries, tiles)),
            dma((count,)), dma((count,)), dma((sections,)), dma((sections,)),
        ],
        compiler_params=pltpu.CompilerParams(
            collective_id=1, has_side_effects=True, vmem_limit_bytes=52 * 2**20
        ),
        name="window",
    )(
        inputs, targets, gain, value_shard, output_shard, input_map, output_map_small, prior,
        padded,
    )


def per_device(
    inputs,
    output_cotangent,
    lengths,
    query_examples,
    norm_gain,
    value_weight,
    output_weight,
    input_projection,
    output_projection,
    fisher_prior,
):
    batches = lengths.shape[0]
    example_rows = inputs.shape[0] // batches
    width = inputs.shape[1]
    positions = jnp.arange(example_rows, dtype=jnp.int32)
    keep = (positions[None, :] < lengths[:, None]).astype(jnp.bfloat16)
    targets = output_cotangent.reshape(batches, example_rows, width) * keep[:, :, None]
    return window(
        inputs.reshape(batches, example_rows, width), targets, norm_gain.astype(jnp.float32),
        value_weight[0], output_weight[0], input_projection[0], output_projection[0],
        fisher_prior[0], query_examples,
    )


def solution(mesh):
    placed = (
        P("dp", None),
        P("dp", None),
        P("dp"),
        P(),
        P("section", None),
        P("section", "dp", None),
        P("section", "dp", None),
        P("section", None, None),
        P("section", None, None),
        P("section", None, None),
    )
    return jax.shard_map(
        per_device, mesh=mesh, in_specs=placed, out_specs=P("dp", None), check_vma=False
    )
```

time: 323 us -> 320 us (level)
  blocking collectives: 36.8 us -> 0 us
  Pallas kernels: 279 us -> 314 us
  local copies, waits for them, and re-layouts: 6.01 us -> 1.24 us
  other arithmetic: 0.26 us -> 4.31 us
    pallas_call x3 -> x1, Pallas kernels: 279 us -> 314 us  [window(): pl.pallas_call(functools.partial(window_kernel, sections, count), out_sha...]
    all_gather x1 -> x0, blocking collectives: 30.5 us -> none  [per_device(): everyone = lax.all_gather(flat, 'dp', axis=0, tiled=True)]
    psum x1 -> x0, blocking collectives: 6.31 us -> none  [per_device(): return lax.psum(section_scores, 'section')]
    unnamed x22 -> x7, local copies, waits for them, and re-layouts: 6 us -> 0.58 us
where the time goes in v1:
time: 320 us; the launch traced here: 319 us
  Pallas kernels  314 us (98%)
  other arithmetic  4.31 us (1%)
    pallas_call x1, Pallas kernels, window(): pl.pallas_call(functools.partial(window_kernel, sections, count), out_sha...  314 us

profile of v1, /device:TPU:0, one launch (start us, length us, event | category | flops | bytes accessed | tf_op | source)
XLA Modules:
  0.0 319.4 jit_solution(13040940213728668373)
XLA Ops:
  0.0 0.7 compare_convert_fusion
  0.7 0.7 dynamic_update_slice.3.queries
  1.4 0.7 convert_element_type.11.gain
  2.1 0.0 copy-start
  2.1 0.0 copy-start.1
  2.1 0.0 copy-start.2
  2.2 2.9 broadcast_multiply_fusion.targets
  5.0 0.0 copy-done
  5.0 0.0 copy-done.1
  5.0 0.0 copy-done.2
  5.0 313.8 %window.1 = f32[2,16]{1,0:T(2,128)S(1)} custom-call(bf16[2,96,4096]{2,1,0:T(8,128)(2,1)} %bitcast.13, bf16[2,96,4096]{2,1,0:T(8,128)(2,1)} %broadcast_multiply_fusion.targets, f32[1,4096]{1,0:T(1,128)S(1)} %convert_element_type.11.gain, bf16[512,1024]{1,0:T(8,128)(2,1)S(1)} %bitcast.8, bf16[512,1024]{1,0:T(8,128)(2,1)} %bitcast.14, ...), custom_call_target="tpu_custom_call" | custom-call | tf_op jit(solution)/shard_map/window/pallas_call | solution.py:608
  318.9 0.6 copy.12
Async XLA Ops:
  2.1 2.9 copy-start
  2.1 2.9 copy-start.1
  2.1 2.9 copy-start.2

commit v2 on v1

--- a/solution.py
+++ b/solution.py
@@ -11,33 +11,76 @@
 HIGHEST = lax.Precision.HIGHEST
 
 
-def inverted(block):
-    size = block.shape[0]
-    rows = lax.broadcasted_iota(jnp.int32, block.shape, 0)
-    columns = lax.broadcasted_iota(jnp.int32, block.shape, 1)
-
-    def sweep(pivot, held):
-        at_row, at_column = rows == pivot, columns == pivot
-        row = jnp.sum(jnp.where(at_row, held, 0.0), axis=0, keepdims=True)
-        column = jnp.sum(jnp.where(at_column, held, 0.0), axis=1, keepdims=True)
-        corner = jnp.sum(jnp.where(at_column[:1], row, 0.0), axis=1, keepdims=True)
-        scale = 1.0 / corner
-        scaled = row * scale
-        updated = held - column * scaled
-        updated = jnp.where(at_row, scaled, updated)
-        updated = jnp.where(at_column, column * scale, updated)
-        return jnp.where(at_row & at_column, -scale, updated)
-
-    return -lax.fori_loop(0, size, sweep, block)
-
-
-def sweep_strip(work, strip, step, block):
-    span = pl.ds(pl.multiple_of(step * block, block), block)
-    corner = inverted(work[span, span])
-    strip[...] = jnp.dot(
-        corner, work[span, :], precision=HIGHEST, preferred_element_type=jnp.float32
+GROUP = 8
+
+
+def small_inverse(held):
+    count = len(held)
+    held = [list(line) for line in held]
+    for pivot in range(count):
+        scale = 1.0 / held[pivot][pivot]
+        line = list(held[pivot])
+        scaled = [value * scale for value in line]
+        for i in range(count):
+            for j in range(i, count):
+                if i != pivot and j != pivot:
+                    held[i][j] = held[j][i] = held[i][j] - line[i] * scaled[j]
+        for j in range(count):
+            held[pivot][j] = held[j][pivot] = scaled[j]
+        held[pivot][pivot] = -scale
+    return [[-value for value in line] for line in held]
+
+
+def sweep_square(square):
+    rows, columns = square.shape
+    lanes = lax.broadcasted_iota(jnp.int32, (GROUP, columns), 1)
+    lines = lax.broadcasted_iota(jnp.int32, (GROUP, columns), 0)
+    wide = lax.broadcasted_iota(jnp.int32, (rows, columns), 1)
+
+    @pl.loop(0, rows // GROUP)
+    def _(at):
+        base = at * GROUP
+        part = pl.ds(pl.multiple_of(base, GROUP), GROUP)
+        panel = square[part, :]
+        corner = [
+            jnp.sum(jnp.where(lanes == base + k, panel, 0.0), axis=1, keepdims=True)
+            for k in range(GROUP)
+        ]
+        spread = [
+            [jnp.broadcast_to(corner[k][i : i + 1, :], (1, columns)) for k in range(GROUP)]
+            for i in range(GROUP)
+        ]
+        inverse = small_inverse(spread)
+        inside = (lanes >= base) & (lanes < base + GROUP)
+        unit = jnp.where(lanes - base == lines, 1.0, 0.0)
+        source = jnp.where(inside, unit, panel)
+        built = []
+        for i in range(GROUP):
+            total = inverse[i][0] * source[:1, :]
+            for k in range(1, GROUP):
+                total = total + inverse[i][k] * source[k : k + 1, :]
+            built.append(total)
+        strip = jnp.concatenate(built, axis=0)
+        signed = jnp.where(inside, -strip, strip)
+        full = square[...]
+        within = (wide >= base) & (wide < base + GROUP)
+        updated = jnp.where(within, 0.0, full)
+        for k in range(GROUP):
+            column = jnp.sum(jnp.where(wide == base + k, full, 0.0), axis=1, keepdims=True)
+            updated = updated - column * signed[k : k + 1, :]
+        square[...] = updated
+        square[part, :] = signed
+
+
+def sweep_strip(work, strip, square, step, block):
+    part = pl.ds(pl.multiple_of(step * block, block), block)
+    square[...] = work[part, part]
+    sweep_square(square)
+    corner = square[...]
+    strip[...] = -jnp.dot(
+        corner, work[part, :], precision=HIGHEST, preferred_element_type=jnp.float32
     )
-    strip[:, span] = -corner
+    strip[:, part] = corner
 
 
 def sweep_rest(work, strip, step, block):
@@ -105,8 +148,8 @@
     sections, count,
     inputs, targets, gain, value_shard, output_shard, input_map, output_map_small, prior, queries,
     scores,
-    weights, work, strip, hidden, following, cotangent, previous, values, upstream, normed,
-    activated, features, factors, squares, gain_half, input_half, first_out, first_in,
+    weights, work, strip, square, small, outer, inner, hidden, following, cotangent, previous, values, upstream, normed,
+    activated, slopes, features, factors, gain_half, input_half, first_out, first_in,
     extra_out, extra_in, second_out, second_in, flats, everyone, rows_all, final,
     gather_send, gather_receive, own_weights, prior_done, entry_own, entry_send, entry_receive,
     forward_send, forward_receive, backward_send, backward_receive,
@@ -118,8 +161,10 @@
     before, after = lax.max(section - 1, 0), lax.min(section + 1, sections - 1)
     side = lax.rem(lax.div(me, PAIR), 2)
     partner = flipped(me, PAIR)
-    batches, length, width = inputs.shape
-    entries = 2 * batches
+    batches, example_length, width = inputs.shape
+    entries, length = hidden.shape[0], hidden.shape[1]
+    per_side = entries // 2
+    cuts = per_side // batches
     half, value_width = weights.shape[1], weights.shape[2]
     rows = value_shard.shape[0]
     piece_rows = rows // PIECES
@@ -173,8 +218,9 @@
         source = (inputs, targets)[kind]
         sink = (hidden, cotangent)[kind]
         wanted = 1 - side if remote else side
-        here = source.at[entry, :, span(2 * part + wanted, stretch)]
-        there = sink.at[side * batches + entry, :, span(part, stretch)]
+        lines = pl.ds((entry % cuts) * length, length)
+        here = source.at[entry // cuts, lines, span(2 * part + wanted, stretch)]
+        there = sink.at[side * per_side + entry, :, span(part, stretch)]
         if not remote:
             return pltpu.make_async_copy(here, there, entry_own.at[kind, entry, part])
         return pltpu.make_async_remote_copy(
@@ -188,7 +234,7 @@
 
     def entry_wait(kind, batch):
         sink = (hidden, cotangent)[kind]
-        owner, entry = lax.div(batch, batches), lax.rem(batch, batches)
+        owner, entry = lax.div(batch, per_side), lax.rem(batch, per_side)
         for part in range(stretches):
             there = sink.at[batch, :, span(part, stretch)]
 
@@ -251,10 +297,6 @@
             device_id_type=MESH,
         )
 
-    def invert_step(step):
-        sweep_strip(work, strip, step, BLOCK)
-        sweep_rest(work, strip, step, BLOCK)
-
     prior_copy = pltpu.make_async_copy(prior, work, prior_done)
     prior_copy.start()
     mine = span(slot_of(me), rows)
@@ -282,7 +324,7 @@
     for kind, wanted in ((0, jnp.logical_not(has_before)), (1, jnp.logical_not(has_after))):
         @pl.when(wanted)
         def _():
-            for entry in range(batches):
+            for entry in range(per_side):
                 for part in range(stretches):
                     entry_copy(kind, entry, part, True).start()
                     entry_copy(kind, entry, part, False).start()
@@ -301,70 +343,63 @@
         here = span(2 * part + side, stretch)
         gain_half[:, there] = gain[:, here]
         input_half[:feature_width, there] = input_map[:, here]
+    for target, shift in ((outer, True), (inner, False)):
+        entry = lax.broadcasted_iota(jnp.int32, target.shape, 1)
+        line = lax.broadcasted_iota(jnp.int32, target.shape, 0)
+        place = lax.div(entry, feature_width) if shift else lax.rem(entry, feature_width)
+        target[...] = jnp.where(place == line, 1.0, 0.0).astype(jnp.bfloat16)
     prior_copy.wait()
 
-    early = min(blocks, PIECES)
-    rest = blocks - early
-
-    @pl.loop(0, PIECES)
+    @pl.loop(0, max(blocks, 2 * PIECES))
     def _(step):
-        @pl.when(step < early)
-        def _():
-            sweep_strip(work, strip, step, BLOCK)
-
-        first = 2 * step
-        serve(lax.div(first, PIECES), lax.rem(first, PIECES))
-
-        @pl.when(step < early)
-        def _():
+        @pl.when(step < blocks)
+        def _():
+            sweep_strip(work, strip, square, step, BLOCK)
             sweep_rest(work, strip, step, BLOCK)
 
-        second = first + 1
-        serve(lax.div(second, PIECES), lax.rem(second, PIECES))
+        @pl.when((step >= 4) & (step < 4 + 2 * PIECES // 2))
+        def _():
+            for extra in range(2):
+                number = lax.min(lax.max((step - 4) * 2 + extra, 0), 2 * PIECES - 1)
+                serve(lax.div(number, PIECES), lax.rem(number, PIECES))
 
     collect(0)
-    edge = lax.div(rest * section, 2 * max(sections - 1, 1))
-
-    @pl.loop(early, early + edge)
-    def _(step):
-        invert_step(step)
-
-    @pl.loop(0, entries)
-    def _(batch):
-        @pl.when(has_before)
-        def _():
-            @pl.loop(0, chunks)
-            def _(piece):
+
+    def forward_first(batch):
+        @pl.when(jnp.logical_not(has_before))
+        def _():
+            entry_wait(0, batch)
+
+        total = jnp.zeros((length, 1), jnp.float32)
+        for piece in range(chunks):
+            columns = pl.ds(piece * chunk, chunk)
+
+            @pl.when(has_before)
+            def _():
                 forward_copy(batch, piece).wait_recv()
 
-        @pl.when(jnp.logical_not(has_before))
-        def _():
-            entry_wait(0, batch)
-
-        @pl.loop(0, length // group)
-        def _(at):
-            part = span(at, group)
-            widened = hidden[batch, part, :].astype(jnp.float32)
-            squares[part, :] = jnp.sum(widened * widened, axis=-1, keepdims=True)
-            normed[part, :] = (widened * gain_half[...]).astype(jnp.bfloat16)
-
-        extras = lax.dot_general(
-            normed[...], input_half[...], CONTRACT_LAST, preferred_element_type=jnp.float32
-        )
-        lanes = lax.broadcasted_iota(jnp.int32, extras.shape, 1)
-        extra_out[batch] = jnp.where(lanes == feature_width, squares[...], extras)
-        extra_copy(batch).start()
-
-        @pl.loop(0, tiles)
-        def _(at):
-            columns = span(at, tile)
+            widened = hidden[batch, :, columns].astype(jnp.float32)
+            total = total + jnp.sum(widened * widened, axis=-1, keepdims=True)
+            normed[:, columns] = (widened * gain_half[:, columns]).astype(jnp.bfloat16)
+
+        for at in range(tiles):
+            columns = pl.ds(at * tile, tile)
             found = jnp.dot(
                 normed[...], value_map[:, columns], preferred_element_type=jnp.float32
             )
             values[batch, :, columns] = found
             first_out[batch, :, columns] = found.astype(jnp.bfloat16)
             first_copy(batch, at).start()
-
+            if at == 0:
+                extras = lax.dot_general(
+                    normed[...], input_half[...], CONTRACT_LAST,
+                    preferred_element_type=jnp.float32,
+                )
+                lanes = lax.broadcasted_iota(jnp.int32, extras.shape, 1)
+                extra_out[batch] = jnp.where(lanes == feature_width, total, extras)
+                extra_copy(batch).start()
+
+    def forward_second(batch):
         extra_copy(batch).wait_recv()
         both = extra_out[batch] + extra_in[batch]
         total = both[:, feature_width : feature_width + 1]
@@ -372,24 +407,18 @@
         factors[batch] = factor
         features[batch] = (both[:, :feature_width] * factor).astype(jnp.bfloat16)
 
-        @pl.loop(0, tiles)
-        def _(at):
-            columns = span(at, tile)
+        for at in range(tiles):
+            columns = pl.ds(at * tile, tile)
             first_copy(batch, at).wait_recv()
             partial = first_in[batch, :, columns].astype(jnp.float32)
-            found = (values[batch, :, columns] + partial) * factors[batch]
+            found = (values[batch, :, columns] + partial) * factor
             values[batch, :, columns] = found
             activated[:, columns] = (found / (1.0 + jnp.exp(-found))).astype(jnp.bfloat16)
 
-        @pl.when(batch == 0)
-        def _():
-            collect(1)
-
         @pl.when(has_after)
         def _():
-            @pl.loop(0, chunks)
-            def _(piece):
-                columns = span(piece, chunk)
+            for piece in range(chunks):
+                columns = pl.ds(piece * chunk, chunk)
                 branch = lax.dot_general(
                     activated[...], output_map[columns, :], CONTRACT_LAST,
                     preferred_element_type=jnp.float32,
@@ -399,53 +428,35 @@
                 ).astype(jnp.bfloat16)
                 forward_copy(batch, piece).start()
 
-    @pl.loop(early + edge, blocks - edge)
-    def _(step):
-        invert_step(step)
-
-    @pl.loop(0, entries)
-    def _(batch):
-        @pl.when(has_after)
-        def _():
-            @pl.loop(0, chunks)
-            def _(piece):
-                backward_copy(batch, piece).wait_recv()
-
-        @pl.when(jnp.logical_not(has_after))
-        def _():
-            entry_wait(1, batch)
-
-        @pl.loop(0, tiles)
-        def _(at):
-            columns = span(at, tile)
+    def backward_first(batch):
+        for at in range(tiles):
+            columns = pl.ds(at * tile, tile)
             found = jnp.dot(
                 cotangent[batch], output_map[:, columns], preferred_element_type=jnp.float32
             )
-            upstream[:, columns] = found
+            upstream[batch, :, columns] = found
             second_out[batch, :, columns] = found.astype(jnp.bfloat16)
             second_copy(batch, at).start()
 
-        slopes = activated
-
-        def slope_tile(at, total):
-            columns = span(at, tile)
+    def backward_second(batch):
+        total = jnp.zeros((length, 1), jnp.float32)
+        for at in range(tiles):
+            columns = pl.ds(at * tile, tile)
             second_copy(batch, at).wait_recv()
-            arrived = upstream[:, columns] + second_in[batch, :, columns].astype(jnp.float32)
+            arrived = upstream[batch, :, columns] + second_in[batch, :, columns].astype(jnp.float32)
             found = values[batch, :, columns]
             logistic = 1.0 / (1.0 + jnp.exp(-found))
             slope = (arrived * logistic * (1.0 + found * (1.0 - logistic))).astype(jnp.bfloat16)
             slopes[:, columns] = slope
-            return total + jnp.sum(slope.astype(jnp.float32) * found, axis=-1, keepdims=True)
-
-        total = lax.fori_loop(0, tiles, slope_tile, jnp.zeros((length, 1), jnp.float32))
+            total = total + jnp.sum(slope.astype(jnp.float32) * found, axis=-1, keepdims=True)
+
         factor = factors[batch]
         shrink = total * (factor * factor) * (1.0 / width)
 
         @pl.when(has_before)
         def _():
-            @pl.loop(0, chunks)
-            def _(piece):
-                columns = span(piece, chunk)
+            for piece in range(chunks):
+                columns = pl.ds(piece * chunk, chunk)
                 normed_grad = lax.dot_general(
                     slopes[...], value_map[columns, :], CONTRACT_LAST,
                     preferred_element_type=jnp.float32,
@@ -462,24 +473,55 @@
         signals = lax.dot_general(
             slopes[...], output_map_small[...], CONTRACT_LAST, preferred_element_type=jnp.float32
         ).astype(jnp.bfloat16)
-        shape = (signal_width, size)
-        entry = lax.broadcasted_iota(jnp.int32, shape, 1)
-        line = lax.broadcasted_iota(jnp.int32, shape, 0)
-        outer = jnp.where(lax.div(entry, feature_width) == line, 1.0, 0.0).astype(jnp.bfloat16)
-        shape = (feature_width, size)
-        entry = lax.broadcasted_iota(jnp.int32, shape, 1)
-        line = lax.broadcasted_iota(jnp.int32, shape, 0)
-        inner = jnp.where(lax.rem(entry, feature_width) == line, 1.0, 0.0).astype(jnp.bfloat16)
-        left = jnp.dot(signals, outer, preferred_element_type=jnp.float32)
-        right = jnp.dot(features[batch], inner, preferred_element_type=jnp.float32)
-        flat = jnp.sum(left * right, axis=0, keepdims=True) * (1.0 / length)
-        flats[lax.div(batch, batches), pl.ds(lax.rem(batch, batches), 1), :] = flat
-
-    @pl.loop(blocks - edge, blocks)
-    def _(step):
-        invert_step(step)
-
-    everyone[me] = flats[side]
+        left = jnp.dot(signals, outer[...], preferred_element_type=jnp.float32)
+        right = jnp.dot(features[batch], inner[...], preferred_element_type=jnp.float32)
+        flat = jnp.sum(left * right, axis=0, keepdims=True) * (1.0 / example_length)
+        flats[lax.div(batch, per_side), pl.ds(lax.rem(batch, per_side), 1), :] = flat
+
+    collect(1)
+
+    @pl.when(jnp.logical_not(has_after))
+    def _():
+        @pl.loop(0, entries)
+        def _(batch):
+            entry_wait(1, batch)
+            backward_first(batch)
+
+    @pl.loop(0, entries + 1)
+    def _(batch):
+        @pl.when(batch < entries)
+        def _():
+            forward_first(lax.min(batch, entries - 1))
+
+        @pl.when(batch > 0)
+        def _():
+            forward_second(lax.max(batch - 1, 0))
+
+            @pl.when(jnp.logical_not(has_after))
+            def _():
+                backward_second(lax.max(batch - 1, 0))
+
+    @pl.when(has_after)
+    def _():
+        @pl.loop(0, entries + 1)
+        def _(batch):
+            @pl.when(batch < entries)
+            def _():
+                for piece in range(chunks):
+                    backward_copy(lax.min(batch, entries - 1), piece).wait_recv()
+
+                backward_first(lax.min(batch, entries - 1))
+
+            @pl.when(batch > 0)
+            def _():
+                backward_second(lax.max(batch - 1, 0))
+
+    ours = flats[side]
+    for entry in range(batches):
+        gathered = ours[entry * cuts : entry * cuts + 1, :]
+        for cut in range(1, cuts):
+            gathered = gathered + ours[entry * cuts + cut : entry * cuts + cut + 1, :]
+        everyone[me, entry : entry + 1, :] = gathered
 
     def publish(offset, origin):
         return pltpu.make_async_remote_copy(
@@ -509,15 +551,18 @@
     )
     shape = (examples, examples)
     diagonal = lax.broadcasted_iota(jnp.int32, shape, 0) == lax.broadcasted_iota(jnp.int32, shape, 1)
-    inverse = inverted(gram + jnp.where(diagonal, 1.0, 0.0))
+    small[...] = jnp.zeros_like(small)
+    small[:, :examples] = gram + jnp.where(diagonal, 1.0, 0.0)
+    sweep_square(small)
+    inverse = -small[:, :examples]
     picked = lax.broadcasted_iota(jnp.int32, (8, examples), 0)
     columns = lax.broadcasted_iota(jnp.int32, (8, examples), 1)
     pick = jnp.where((columns == me * batches + picked) & (picked < batches), 1.0, 0.0)
     owners = lax.broadcasted_iota(jnp.int32, (examples, queries.shape[1]), 0)
     selector = jnp.where(owners == queries[...], 1.0, 0.0)
-    ours = jnp.dot(pick, gram, precision=HIGHEST, preferred_element_type=jnp.float32)
+    picked_gram = jnp.dot(pick, gram, precision=HIGHEST, preferred_element_type=jnp.float32)
     chosen = jnp.dot(inverse, selector, precision=HIGHEST, preferred_element_type=jnp.float32)
-    final[section] = jnp.dot(ours, chosen, precision=HIGHEST, preferred_element_type=jnp.float32)
+    final[section] = jnp.dot(picked_gram, chosen, precision=HIGHEST, preferred_element_type=jnp.float32)
 
     def finish(offset, origin):
         return pltpu.make_async_remote_copy(
@@ -553,7 +598,7 @@
     for kind, wanted in ((0, jnp.logical_not(has_before)), (1, jnp.logical_not(has_after))):
         @pl.when(wanted)
         def _():
-            for entry in range(batches):
+            for entry in range(per_side):
                 for part in range(stretches):
                     entry_copy(kind, entry, part, True).wait_send()
 
@@ -587,16 +632,19 @@
     inputs, targets, gain, value_shard, output_shard, input_map, output_map_small, prior, queries
 ):
     sections, count = lax.axis_size("section"), lax.axis_size("dp")
-    batches, length, width = inputs.shape
+    batches, example_length, width = inputs.shape
     rows, value_width = value_shard.shape
-    entries = 2 * batches
+    cuts = 1
+    length = example_length // cuts
+    entries = 2 * batches * cuts
     half = width // 2
     size = prior.shape[0]
     feature_width = input_map.shape[0]
+    signal_width = output_map_small.shape[0]
     asked = queries.shape[0]
     padded = jnp.full((1, LANES * pl.cdiv(asked, LANES)), -1, jnp.int32)
     padded = lax.dynamic_update_slice(padded, queries[None, :], (0, 0))
-    chunks, tiles = 8, 4
+    chunks, tiles = 4, 2
     events = len(gather_events(count))
     stretches = half // (PAIR * rows)
     dma = pltpu.SemaphoreType.DMA
@@ -616,24 +664,28 @@
             pltpu.VMEM((2, half, value_width), jnp.bfloat16),
             pltpu.VMEM((size, size), jnp.float32),
             pltpu.VMEM((BLOCK, size), jnp.float32),
+            pltpu.VMEM((BLOCK, BLOCK), jnp.float32),
+            pltpu.VMEM((count * batches, LANES), jnp.float32),
+            pltpu.VMEM((signal_width, size), jnp.bfloat16),
+            pltpu.VMEM((feature_width, size), jnp.bfloat16),
             stream, stream, stream, stream,
             pltpu.VMEM((entries, length, value_width), jnp.float32),
-            pltpu.VMEM((length, value_width), jnp.float32),
+            pltpu.VMEM((entries, length, value_width), jnp.float32),
             pltpu.VMEM((length, half), jnp.bfloat16),
+            pltpu.VMEM((length, value_width), jnp.bfloat16),
             pltpu.VMEM((length, value_width), jnp.bfloat16),
             pltpu.VMEM((entries, length, feature_width), jnp.bfloat16),
             pltpu.VMEM((entries, length, 1), jnp.float32),
-            pltpu.VMEM((length, 1), jnp.float32),
             pltpu.VMEM((1, half), jnp.float32),
             pltpu.VMEM((LANES, half), jnp.bfloat16),
             parts, parts, extra, extra, parts, parts,
-            pltpu.VMEM((2, batches, size), jnp.float32),
+            pltpu.VMEM((2, batches * cuts, size), jnp.float32),
             pltpu.VMEM((count, batches, size), jnp.float32),
             pltpu.VMEM((count * batches, size), jnp.float32),
             pltpu.VMEM((sections, 8, padded.shape[1]), jnp.float32),
             dma((events, 2, PIECES)), dma((events, 2, PIECES)), dma((2,)), dma,
-            dma((2, batches, stretches)), dma((2, batches, stretches)),
-            dma((2, batches, stretches)),
+            dma((2, batches * cuts, stretches)), dma((2, batches * cuts, stretches)),
+            dma((2, batches * cuts, stretches)),
             dma((entries, chunks)), dma((entries, chunks)),
             dma((entries, chunks)), dma((entries, chunks)),
             dma((entries, tiles)), dma((entries, tiles)), dma((entries,)), dma((entries,)),

time: 320 us -> 215 us (0.67)
  Pallas kernels: 314 us -> 209 us
    pallas_call x1, Pallas kernels: 314 us -> 209 us  [window(): pl.pallas_call(functools.partial(window_kernel, sections, count), out_sha...]
where the time goes in v2:
time: 215 us; the launch traced here: 214 us
  Pallas kernels  209 us (97%)
  other arithmetic  4.31 us (2%)
    pallas_call x1, Pallas kernels, window(): pl.pallas_call(functools.partial(window_kernel, sections, count), out_sha...  209 us

profile of v2, /device:TPU:0, one launch (start us, length us, event | category | flops | bytes accessed | tf_op | source)
XLA Modules:
  0.0 214.4 jit_solution(3763768391549543798)
XLA Ops:
  0.0 0.7 compare_convert_fusion
  0.7 0.7 dynamic_update_slice.3.queries
  1.4 0.7 convert_element_type.11.gain
  2.1 0.0 copy-start
  2.1 0.0 copy-start.1
  2.1 0.0 copy-start.2
  2.2 2.9 %broadcast_multiply_fusion.targets = bf16[2,96,4096]{2,1,0:T(8,128)(2,1)} fusion(bf16[2,96,4096]{2,1,0:T(8,128)(2,1)} %bitcast.12, bf16[2,96]{1,0:T(2,128)(2,1)S(1)} %compare_convert_fusion), kind=kLoop, calls=%fused_computation | loop fusion | flops 786432 | bytes 3146112 | tf_op jit(solution)/shard_map/mul | solution.py:722
  5.0 0.0 copy-done
  5.0 0.0 copy-done.1
  5.0 0.0 copy-done.2
  5.0 208.8 %window.1 = f32[2,16]{1,0:T(2,128)S(1)} custom-call(bf16[2,96,4096]{2,1,0:T(8,128)(2,1)} %bitcast.13, bf16[2,96,4096]{2,1,0:T(8,128)(2,1)} %broadcast_multiply_fusion.targets, f32[1,4096]{1,0:T(1,128)S(1)} %convert_element_type.11.gain, bf16[512,1024]{1,0:T(8,128)(2,1)S(1)} %bitcast.8, bf16[512,1024]{1,0:T(8,128)(2,1)} %bitcast.14, ...), custom_call_target="tpu_custom_call" | custom-call | tf_op jit(solution)/shard_map/window/pallas_call | solution.py:656
  213.8 0.6 copy.12
Async XLA Ops:
  2.1 2.9 %copy-start = (bf16[1,512,1024]{2,1,0:T(8,128)(2,1)S(1)}, bf16[1,512,1024]{2,1,0:T(8,128)(2,1)}, u32[]{:S(2)}) copy-start(bf16[1,512,1024]{2,1,0:T(8,128)(2,1)} %param.15) | copy-start | bytes 3145732
  2.1 2.9 %copy-start.1 = (bf16[1,32,4096]{2,1,0:T(8,128)(2,1)S(1)}, bf16[1,32,4096]{2,1,0:T(8,128)(2,1)}, u32[]{:S(2)}) copy-start(bf16[1,32,4096]{2,1,0:T(8,128)(2,1)} %param.17) | copy-start | bytes 786436
  2.1 2.9 %copy-start.2 = (bf16[1,32,1024]{2,1,0:T(8,128)(2,1)S(1)}, bf16[1,32,1024]{2,1,0:T(8,128)(2,1)}, u32[]{:S(2)}) copy-start(bf16[1,32,1024]{2,1,0:T(8,128)(2,1)} %param.18) | copy-start | bytes 196612

commit v3 on v2

--- a/solution.py
+++ b/solution.py
@@ -105,6 +105,9 @@
 CONTRACT_LAST = (((1,), (1,)), ((), ()))
 PAIR = 2
 PIECES = 4
+LAG = 4
+LEAD = 3
+RATE = 2
 BLOCK = 128
 LANES = 128
 
@@ -146,20 +149,23 @@
 
 def window_kernel(
     sections, count,
-    inputs, targets, gain, value_shard, output_shard, input_map, output_map_small, prior, queries,
-    scores,
+    inputs, targets, gain, lengths, value_shard, output_shard, input_map, output_map_small, prior,
+    queries, scores,
     weights, work, strip, square, small, outer, inner, hidden, following, cotangent, previous, values, upstream, normed,
     activated, slopes, features, factors, gain_half, input_half, first_out, first_in,
-    extra_out, extra_in, second_out, second_in, flats, everyone, rows_all, final,
-    gather_send, gather_receive, own_weights, prior_done, entry_own, entry_send, entry_receive,
+    extra_own, extra_out, extra_in, staging, second_out, second_in, flats, everyone, rows_all, final,
+    gather_send, gather_receive, own_weights, prior_done, staged, entry_own, entry_send, entry_receive,
     forward_send, forward_receive, backward_send, backward_receive,
     first_send, first_receive, extra_send, extra_receive, second_send, second_receive,
-    publish_send, publish_receive, final_send, final_receive,
+    publish_send, publish_receive, final_send, final_receive, turn,
 ):
     section, me = lax.axis_index("section"), lax.axis_index("dp")
     has_before, has_after = section > 0, section < sections - 1
     before, after = lax.max(section - 1, 0), lax.min(section + 1, sections - 1)
     side = lax.rem(lax.div(me, PAIR), 2)
+    follows = lax.rem(section, 2) == 1
+    leads = jnp.logical_not(follows)
+    twin = section + 1 - 2 * lax.rem(section, 2)
     partner = flipped(me, PAIR)
     batches, example_length, width = inputs.shape
     entries, length = hidden.shape[0], hidden.shape[1]
@@ -197,6 +203,13 @@
             device_id_type=MESH,
         )
 
+    def start_gather():
+        for array in range(2):
+            for piece in range(PIECES):
+                for number, (_, mask) in enumerate(events):
+                    if mask == 0:
+                        gather_copy(number, array, piece, True).start()
+
     def serve(array, piece):
         for number, (bit, mask) in enumerate(events):
             forwards = [later for later, (_, want) in enumerate(events) if want == bit | mask]
@@ -215,7 +228,7 @@
         kept[array].wait()
 
     def entry_copy(kind, entry, part, remote):
-        source = (inputs, targets)[kind]
+        source = (inputs, staging)[kind]
         sink = (hidden, cotangent)[kind]
         wanted = 1 - side if remote else side
         lines = pl.ds((entry % cuts) * length, length)
@@ -299,6 +312,12 @@
 
     prior_copy = pltpu.make_async_copy(prior, work, prior_done)
     prior_copy.start()
+    stage_copy = pltpu.make_async_copy(targets, staging, staged)
+
+    @pl.when(jnp.logical_not(has_after))
+    def _():
+        stage_copy.start()
+
     mine = span(slot_of(me), rows)
     kept = [
         pltpu.make_async_copy(shards[array], weights.at[array, mine, :], own_weights.at[array])
@@ -321,19 +340,30 @@
 
     pl.semaphore_wait(barrier, count + sections - 2)
 
-    for kind, wanted in ((0, jnp.logical_not(has_before)), (1, jnp.logical_not(has_after))):
-        @pl.when(wanted)
-        def _():
-            for entry in range(per_side):
-                for part in range(stretches):
-                    entry_copy(kind, entry, part, True).start()
-                    entry_copy(kind, entry, part, False).start()
-
-    for array in range(2):
-        for piece in range(PIECES):
-            for number, (_, mask) in enumerate(events):
-                if mask == 0:
-                    gather_copy(number, array, piece, True).start()
+    @pl.when(leads)
+    def _():
+        start_gather()
+
+    def start_entries(kind):
+        for entry in range(per_side):
+            for part in range(stretches):
+                entry_copy(kind, entry, part, True).start()
+                entry_copy(kind, entry, part, False).start()
+
+    @pl.when(jnp.logical_not(has_before))
+    def _():
+        start_entries(0)
+
+    @pl.when(jnp.logical_not(has_after))
+    def _():
+        stage_copy.wait()
+        line = lax.broadcasted_iota(jnp.int32, (example_length, 1), 0)
+        for entry in range(batches):
+            live = jnp.where(line < lengths[:, entry : entry + 1], 1.0, 0.0)
+            staging[entry] = staging[entry] * live.astype(jnp.bfloat16)
+
+        start_entries(1)
+
     for copy in kept:
         copy.start()
 
@@ -341,7 +371,7 @@
     for part in range(stretches):
         there = pl.ds(part * stretch, stretch)
         here = span(2 * part + side, stretch)
-        gain_half[:, there] = gain[:, here]
+        gain_half[:, there] = gain[:, here].astype(jnp.float32)
         input_half[:feature_width, there] = input_map[:, here]
     for target, shift in ((outer, True), (inner, False)):
         entry = lax.broadcasted_iota(jnp.int32, target.shape, 1)
@@ -350,20 +380,56 @@
         target[...] = jnp.where(place == line, 1.0, 0.0).astype(jnp.bfloat16)
     prior_copy.wait()
 
-    @pl.loop(0, max(blocks, 2 * PIECES))
+    def sweep(step):
+        sweep_strip(work, strip, square, step, BLOCK)
+        sweep_rest(work, strip, step, BLOCK)
+
+    late = lax.rem(section, 2) * LAG
+    served = pl.cdiv(LEAD + pl.cdiv(2 * PIECES, RATE), 2)
+    stop = lax.min(late + served, blocks)
+
+    def serve_at(point):
+        for extra in range(RATE):
+            number = point * RATE + extra
+
+            @pl.when((number >= 0) & (number < 2 * PIECES))
+            def _():
+                bounded = lax.min(lax.max(number, 0), 2 * PIECES - 1)
+                serve(lax.div(bounded, PIECES), lax.rem(bounded, PIECES))
+
+    @pl.loop(0, late + served)
     def _(step):
+        @pl.when(follows & (step == LAG))
+        def _():
+            pl.semaphore_wait(turn, 1)
+            start_gather()
+
+        point = 2 * (step - late) - LEAD
+
         @pl.when(step < blocks)
         def _():
             sweep_strip(work, strip, square, step, BLOCK)
+
+        serve_at(point)
+
+        @pl.when(step < blocks)
+        def _():
             sweep_rest(work, strip, step, BLOCK)
 
-        @pl.when((step >= 4) & (step < 4 + 2 * PIECES // 2))
-        def _():
-            for extra in range(2):
-                number = lax.min(lax.max((step - 4) * 2 + extra, 0), 2 * PIECES - 1)
-                serve(lax.div(number, PIECES), lax.rem(number, PIECES))
+        serve_at(point + 1)
 
     collect(0)
+    collect(1)
+
+    @pl.when(leads)
+    def _():
+        pl.semaphore_signal(turn, inc=1, device_id={"section": twin}, device_id_type=MESH)
+
+    first_stop = lax.select(has_before, blocks, stop)
+
+    @pl.loop(stop, first_stop)
+    def _(step):
+        sweep(step)
 
     def forward_first(batch):
         @pl.when(jnp.logical_not(has_before))
@@ -396,13 +462,21 @@
                     preferred_element_type=jnp.float32,
                 )
                 lanes = lax.broadcasted_iota(jnp.int32, extras.shape, 1)
-                extra_out[batch] = jnp.where(lanes == feature_width, total, extras)
+                extra_own[batch] = jnp.where(lanes == feature_width, total, extras)
+                high = total.astype(jnp.bfloat16).astype(jnp.float32)
+                extras = jnp.where(lanes == feature_width, high, extras)
+                extras = jnp.where(lanes == feature_width + 1, total - high, extras)
+                extra_out[batch] = extras.astype(jnp.bfloat16)
                 extra_copy(batch).start()
 
     def forward_second(batch):
         extra_copy(batch).wait_recv()
-        both = extra_out[batch] + extra_in[batch]
-        total = both[:, feature_width : feature_width + 1]
+        arrived = extra_in[batch].astype(jnp.float32)
+        both = extra_own[batch] + arrived
+        total = (
+            both[:, feature_width : feature_width + 1]
+            + arrived[:, feature_width + 1 : feature_width + 2]
+        )
         factor = lax.rsqrt(total * (1.0 / width) + 1e-05)
         factors[batch] = factor
         features[batch] = (both[:, :feature_width] * factor).astype(jnp.bfloat16)
@@ -478,8 +552,6 @@
         flat = jnp.sum(left * right, axis=0, keepdims=True) * (1.0 / example_length)
         flats[lax.div(batch, per_side), pl.ds(lax.rem(batch, per_side), 1), :] = flat
 
-    collect(1)
-
     @pl.when(jnp.logical_not(has_after))
     def _():
         @pl.loop(0, entries)
@@ -500,6 +572,10 @@
             @pl.when(jnp.logical_not(has_after))
             def _():
                 backward_second(lax.max(batch - 1, 0))
+
+    @pl.loop(first_stop, blocks)
+    def _(step):
+        sweep(step)
 
     @pl.when(has_after)
     def _():
@@ -629,7 +705,7 @@
 
 
 def window(
-    inputs, targets, gain, value_shard, output_shard, input_map, output_map_small, prior, queries
+    inputs, targets, gain, lengths, value_shard, output_shard, input_map, output_map_small, prior, queries
 ):
     sections, count = lax.axis_size("section"), lax.axis_size("dp")
     batches, example_length, width = inputs.shape
@@ -642,22 +718,21 @@
     feature_width = input_map.shape[0]
     signal_width = output_map_small.shape[0]
     asked = queries.shape[0]
-    padded = jnp.full((1, LANES * pl.cdiv(asked, LANES)), -1, jnp.int32)
-    padded = lax.dynamic_update_slice(padded, queries[None, :], (0, 0))
     chunks, tiles = 4, 2
     events = len(gather_events(count))
     stretches = half // (PAIR * rows)
     dma = pltpu.SemaphoreType.DMA
     stream = pltpu.VMEM((entries, length, half), jnp.bfloat16)
     parts = pltpu.VMEM((entries, length, value_width), jnp.bfloat16)
-    extra = pltpu.VMEM((entries, length, LANES), jnp.float32)
+    extra = pltpu.VMEM((entries, length, LANES), jnp.bfloat16)
     anywhere = pl.BlockSpec(memory_space=pl.ANY)
     inside = pl.BlockSpec(memory_space=pltpu.VMEM)
     return pl.pallas_call(
         functools.partial(window_kernel, sections, count),
         out_shape=jax.ShapeDtypeStruct((batches, asked), jnp.float32),
         in_specs=[
-            anywhere, anywhere, inside, anywhere, anywhere, inside, inside, anywhere, inside
+            anywhere, anywhere, inside, inside, anywhere, anywhere, inside, inside, anywhere,
+            inside,
         ],
         out_specs=inside,
         scratch_shapes=[
@@ -678,12 +753,13 @@
             pltpu.VMEM((entries, length, 1), jnp.float32),
             pltpu.VMEM((1, half), jnp.float32),
             pltpu.VMEM((LANES, half), jnp.bfloat16),
-            parts, parts, extra, extra, parts, parts,
+            parts, parts, pltpu.VMEM((entries, length, LANES), jnp.float32), extra, extra,
+            pltpu.VMEM((batches, example_length, width), jnp.bfloat16), parts, parts,
             pltpu.VMEM((2, batches * cuts, size), jnp.float32),
             pltpu.VMEM((count, batches, size), jnp.float32),
             pltpu.VMEM((count * batches, size), jnp.float32),
-            pltpu.VMEM((sections, 8, padded.shape[1]), jnp.float32),
-            dma((events, 2, PIECES)), dma((events, 2, PIECES)), dma((2,)), dma,
+            pltpu.VMEM((sections, 8, asked), jnp.float32),
+            dma((events, 2, PIECES)), dma((events, 2, PIECES)), dma((2,)), dma, dma,
             dma((2, batches * cuts, stretches)), dma((2, batches * cuts, stretches)),
             dma((2, batches * cuts, stretches)),
             dma((entries, chunks)), dma((entries, chunks)),
@@ -691,14 +767,15 @@
             dma((entries, tiles)), dma((entries, tiles)), dma((entries,)), dma((entries,)),
             dma((entries, tiles)), dma((entries, tiles)),
             dma((count,)), dma((count,)), dma((sections,)), dma((sections,)),
+            pltpu.SemaphoreType.REGULAR,
         ],
         compiler_params=pltpu.CompilerParams(
             collective_id=1, has_side_effects=True, vmem_limit_bytes=52 * 2**20
         ),
         name="window",
     )(
-        inputs, targets, gain, value_shard, output_shard, input_map, output_map_small, prior,
-        padded,
+        inputs, targets, gain, lengths, value_shard, output_shard, input_map, output_map_small,
+        prior, queries[None, :],
     )
 
 
@@ -717,11 +794,9 @@
     batches = lengths.shape[0]
     example_rows = inputs.shape[0] // batches
     width = inputs.shape[1]
-    positions = jnp.arange(example_rows, dtype=jnp.int32)
-    keep = (positions[None, :] < lengths[:, None]).astype(jnp.bfloat16)
-    targets = output_cotangent.reshape(batches, example_rows, width) * keep[:, :, None]
+    targets = output_cotangent.reshape(batches, example_rows, width)
     return window(
-        inputs.reshape(batches, example_rows, width), targets, norm_gain.astype(jnp.float32),
+        inputs.reshape(batches, example_rows, width), targets, norm_gain, lengths[None, :],
         value_weight[0], output_weight[0], input_projection[0], output_projection[0],
         fisher_prior[0], query_examples,
     )

time: 215 us -> 200 us (0.930)
  Pallas kernels: 209 us -> 195 us
  local copies, waits for them, and re-layouts: 1.24 us -> 5.6 us
  other arithmetic: 4.31 us -> 0 us
    pallas_call x1, Pallas kernels: 209 us -> 195 us  [window(): pl.pallas_call(functools.partial(window_kernel, sections, count), out_sha...]
    unnamed x7 -> x13, local copies, waits for them, and re-layouts: 0.58 us -> 5.6 us
    mul x1 -> x0, other arithmetic: 2.86 us -> none  [per_device(): output_cotangent.reshape(batches, example_rows, width) * keep[:, :, None]]
where the time goes in v3:
time: 200 us
  Pallas kernels  195 us (98%)
  local copies, waits for them, and re-layouts  5.6 us (3%)
    pallas_call x1, Pallas kernels, window(): pl.pallas_call(functools.partial(window_kernel, sections, count), out_sha...  195 us
    unnamed x13, local copies, waits for them, and re-layouts  5.6 us

profile of v3, /device:TPU:0, one launch (start us, length us, event | category | flops | bytes accessed | tf_op | source)
XLA Modules:
  0.0 200.2 jit_solution(10966684697249095444)
XLA Ops:
  0.0 0.0 copy-start
  0.0 1.2 copy-done
  1.2 0.0 copy-start.1
  1.2 0.9 copy-done.1
  2.2 0.0 copy-start.2
  2.2 0.8 copy-done.2
  3.0 0.0 copy-start.3
  3.0 0.7 copy-done.3
  3.7 0.0 copy-start.4
  3.7 0.7 copy-done.4
  4.4 0.0 copy-start.5
  4.4 0.7 copy-done.5
  5.0 194.5 %window.1 = f32[2,16]{1,0:T(2,128)S(1)} custom-call(bf16[2,96,4096]{2,1,0:T(8,128)(2,1)} %bitcast.15, bf16[2,96,4096]{2,1,0:T(8,128)(2,1)} %bitcast.16, bf16[1,4096]{1,0:T(2,128)(2,1)S(1)} %copy-done.3, s32[1,2]{1,0:T(1,128)S(1)} %bitcast.12, bf16[512,1024]{1,0:T(8,128)(2,1)S(1)} %bitcast.9, bf16[512,1024]{1,0:T(8,128)(2,1)} %bitcast.17, ...), custom_call_target="tpu_custom_call" | custom-call | tf_op jit(solution)/shard_map/window/pallas_call | solution.py:730
  199.6 0.6 copy.12
Async XLA Ops:
  0.0 1.2 copy-start
  1.2 0.9 copy-start.1
  2.2 0.8 copy-start.2
  3.0 0.7 copy-start.3
  3.7 0.7 copy-start.4
  4.4 0.7 copy-start.5

commit v4 on v3

--- a/solution.py
+++ b/solution.py
@@ -105,6 +105,8 @@
 CONTRACT_LAST = (((1,), (1,)), ((), ()))
 PAIR = 2
 PIECES = 4
+EAGER = 1
+AHEAD = 2
 LAG = 4
 LEAD = 3
 RATE = 2
@@ -149,8 +151,9 @@
 
 def window_kernel(
     sections, count,
-    inputs, targets, gain, lengths, value_shard, output_shard, input_map, output_map_small, prior,
-    queries, scores,
+    inputs, targets, gain_kept, lengths_kept, value_shard, output_shard, input_kept, output_kept,
+    prior, queries_kept, scores,
+    gain, lengths, input_map, output_map_small, queries, small_done,
     weights, work, strip, square, small, outer, inner, hidden, following, cotangent, previous, values, upstream, normed,
     activated, slopes, features, factors, gain_half, input_half, first_out, first_in,
     extra_own, extra_out, extra_in, staging, second_out, second_in, flats, everyone, rows_all, final,
@@ -310,6 +313,15 @@
             device_id_type=MESH,
         )
 
+    small_copies = [
+        pltpu.make_async_copy(source, sink, small_done.at[number])
+        for number, (source, sink) in enumerate((
+            (gain_kept, gain), (lengths_kept, lengths), (input_kept, input_map),
+            (output_kept, output_map_small), (queries_kept, queries),
+        ))
+    ]
+    for copy in small_copies:
+        copy.start()
     prior_copy = pltpu.make_async_copy(prior, work, prior_done)
     prior_copy.start()
     stage_copy = pltpu.make_async_copy(targets, staging, staged)
@@ -353,6 +365,9 @@
     @pl.when(jnp.logical_not(has_before))
     def _():
         start_entries(0)
+
+    for copy in small_copies:
+        copy.wait()
 
     @pl.when(jnp.logical_not(has_after))
     def _():
@@ -379,57 +394,6 @@
         place = lax.div(entry, feature_width) if shift else lax.rem(entry, feature_width)
         target[...] = jnp.where(place == line, 1.0, 0.0).astype(jnp.bfloat16)
     prior_copy.wait()
-
-    def sweep(step):
-        sweep_strip(work, strip, square, step, BLOCK)
-        sweep_rest(work, strip, step, BLOCK)
-
-    late = lax.rem(section, 2) * LAG
-    served = pl.cdiv(LEAD + pl.cdiv(2 * PIECES, RATE), 2)
-    stop = lax.min(late + served, blocks)
-
-    def serve_at(point):
-        for extra in range(RATE):
-            number = point * RATE + extra
-
-            @pl.when((number >= 0) & (number < 2 * PIECES))
-            def _():
-                bounded = lax.min(lax.max(number, 0), 2 * PIECES - 1)
-                serve(lax.div(bounded, PIECES), lax.rem(bounded, PIECES))
-
-    @pl.loop(0, late + served)
-    def _(step):
-        @pl.when(follows & (step == LAG))
-        def _():
-            pl.semaphore_wait(turn, 1)
-            start_gather()
-
-        point = 2 * (step - late) - LEAD
-
-        @pl.when(step < blocks)
-        def _():
-            sweep_strip(work, strip, square, step, BLOCK)
-
-        serve_at(point)
-
-        @pl.when(step < blocks)
-        def _():
-            sweep_rest(work, strip, step, BLOCK)
-
-        serve_at(point + 1)
-
-    collect(0)
-    collect(1)
-
-    @pl.when(leads)
-    def _():
-        pl.semaphore_signal(turn, inc=1, device_id={"section": twin}, device_id_type=MESH)
-
-    first_stop = lax.select(has_before, blocks, stop)
-
-    @pl.loop(stop, first_stop)
-    def _(step):
-        sweep(step)
 
     def forward_first(batch):
         @pl.when(jnp.logical_not(has_before))
@@ -552,6 +516,68 @@
         flat = jnp.sum(left * right, axis=0, keepdims=True) * (1.0 / example_length)
         flats[lax.div(batch, per_side), pl.ds(lax.rem(batch, per_side), 1), :] = flat
 
+    def sweep(step):
+        sweep_strip(work, strip, square, step, BLOCK)
+        sweep_rest(work, strip, step, BLOCK)
+
+    late = lax.rem(section, 2) * LAG
+    served = pl.cdiv(LEAD + pl.cdiv(2 * PIECES, RATE), 2)
+    stop = lax.min(late + served, blocks)
+
+    def serve_at(point):
+        for extra in range(RATE):
+            number = point * RATE + extra
+
+            @pl.when((number >= 0) & (number < 2 * PIECES))
+            def _():
+                bounded = lax.min(lax.max(number, 0), 2 * PIECES - 1)
+                serve(lax.div(bounded, PIECES), lax.rem(bounded, PIECES))
+
+    @pl.loop(0, late + served)
+    def _(step):
+        @pl.when(follows & (step == LAG))
+        def _():
+            pl.semaphore_wait(turn, 1)
+            start_gather()
+
+        point = 2 * (step - late) - LEAD
+
+        @pl.when(step < blocks)
+        def _():
+            sweep_strip(work, strip, square, step, BLOCK)
+
+        @pl.when((section == EAGER) & (step == late + served - 1))
+        def _():
+            collect(0)
+
+            @pl.loop(0, AHEAD)
+            def _(batch):
+                forward_first(batch)
+
+        serve_at(point)
+
+        @pl.when(step < blocks)
+        def _():
+            sweep_rest(work, strip, step, BLOCK)
+
+        serve_at(point + 1)
+
+    @pl.when(section != EAGER)
+    def _():
+        collect(0)
+
+    collect(1)
+
+    @pl.when(leads)
+    def _():
+        pl.semaphore_signal(turn, inc=1, device_id={"section": twin}, device_id_type=MESH)
+
+    first_stop = lax.select(has_before, blocks, stop)
+
+    @pl.loop(stop, first_stop)
+    def _(step):
+        sweep(step)
+
     @pl.when(jnp.logical_not(has_after))
     def _():
         @pl.loop(0, entries)
@@ -561,7 +587,7 @@
 
     @pl.loop(0, entries + 1)
     def _(batch):
-        @pl.when(batch < entries)
+        @pl.when((batch < entries) & ((section != EAGER) | (batch >= AHEAD)))
         def _():
             forward_first(lax.min(batch, entries - 1))
 
@@ -731,11 +757,17 @@
         functools.partial(window_kernel, sections, count),
         out_shape=jax.ShapeDtypeStruct((batches, asked), jnp.float32),
         in_specs=[
-            anywhere, anywhere, inside, inside, anywhere, anywhere, inside, inside, anywhere,
-            inside,
+            anywhere, anywhere, anywhere, anywhere, anywhere, anywhere, anywhere, anywhere,
+            anywhere, anywhere,
         ],
         out_specs=inside,
         scratch_shapes=[
+            pltpu.VMEM(gain.shape, gain.dtype),
+            pltpu.VMEM(lengths.shape, lengths.dtype),
+            pltpu.VMEM(input_map.shape, input_map.dtype),
+            pltpu.VMEM(output_map_small.shape, output_map_small.dtype),
+            pltpu.VMEM((1, asked), queries.dtype),
+            dma((5,)),
             pltpu.VMEM((2, half, value_width), jnp.bfloat16),
             pltpu.VMEM((size, size), jnp.float32),
             pltpu.VMEM((BLOCK, size), jnp.float32),
@@ -770,7 +802,7 @@
             pltpu.SemaphoreType.REGULAR,
         ],
         compiler_params=pltpu.CompilerParams(
-            collective_id=1, has_side_effects=True, vmem_limit_bytes=52 * 2**20
+            collective_id=1, has_side_effects=True, vmem_limit_bytes=67_000_000
         ),
         name="window",
     )(

time: 200 us -> 193 us (0.965)
  local copies, waits for them, and re-layouts: 5.6 us -> 1.24 us
  Pallas kernels: 195 us -> 191 us
    unnamed x13 -> x1, local copies, waits for them, and re-layouts: 5.6 us -> 1.24 us
    pallas_call x1, Pallas kernels: 195 us -> 191 us  [window(): pl.pallas_call(functools.partial(window_kernel, sections, count), out_sha...]
where the time goes in v4:
time: 193 us
  Pallas kernels  191 us (99%)
    pallas_call x1, Pallas kernels, window(): pl.pallas_call(functools.partial(window_kernel, sections, count), out_sha...  191 us

profile of v4, /device:TPU:0, one launch (start us, length us, event | category | flops | bytes accessed | tf_op | source)
XLA Modules:
  0.0 192.7 jit_solution(16327991455597967041)
XLA Ops:
  0.0 191.4 %window.1 = f32[2,16]{1,0:T(2,128)} custom-call(bf16[2,96,4096]{2,1,0:T(8,128)(2,1)} %bitcast.10, bf16[2,96,4096]{2,1,0:T(8,128)(2,1)} %bitcast.11, bf16[1,4096]{1,0:T(2,128)(2,1)} %gain_kept.1, s32[1,2]{1,0:T(1,128)} %bitcast.16, bf16[512,1024]{1,0:T(8,128)(2,1)} %bitcast.12, bf16[512,1024]{1,0:T(8,128)(2,1)} %bitcast.13, bf16[32,4096]{1,0:T(8,128)(2,1)} %bitcast.14, ...), custom_call_target="tpu_custom_call" | custom-call | tf_op jit(solution)/shard_map/window/pallas_call | solution.py:756
  191.4 1.2 copy.12

commit v5 on v4

--- a/solution.py
+++ b/solution.py
@@ -105,6 +105,7 @@
 CONTRACT_LAST = (((1,), (1,)), ((), ()))
 PAIR = 2
 PIECES = 4
+TURN = 256
 EAGER = 1
 AHEAD = 2
 LAG = 4
@@ -154,7 +155,7 @@
     inputs, targets, gain_kept, lengths_kept, value_shard, output_shard, input_kept, output_kept,
     prior, queries_kept, scores,
     gain, lengths, input_map, output_map_small, queries, small_done,
-    weights, work, strip, square, small, outer, inner, hidden, following, cotangent, previous, values, upstream, normed,
+    weights, turned, work, strip, square, small, outer, inner, hidden, following, cotangent, previous, values, upstream, normed,
     activated, slopes, features, factors, gain_half, input_half, first_out, first_in,
     extra_own, extra_out, extra_in, staging, second_out, second_in, flats, everyone, rows_all, final,
     gather_send, gather_receive, own_weights, prior_done, staged, entry_own, entry_send, entry_receive,
@@ -395,6 +396,12 @@
         target[...] = jnp.where(place == line, 1.0, 0.0).astype(jnp.bfloat16)
     prior_copy.wait()
 
+    def turn_over():
+        @pl.loop(0, half // TURN)
+        def _(at):
+            part = span(at, TURN)
+            turned[:, part] = value_map[part, :].T
+
     def forward_first(batch):
         @pl.when(jnp.logical_not(has_before))
         def _():
@@ -495,9 +502,8 @@
         def _():
             for piece in range(chunks):
                 columns = pl.ds(piece * chunk, chunk)
-                normed_grad = lax.dot_general(
-                    slopes[...], value_map[columns, :], CONTRACT_LAST,
-                    preferred_element_type=jnp.float32,
+                normed_grad = jnp.dot(
+                    slopes[...], turned[:, columns], preferred_element_type=jnp.float32
                 )
                 weighted = normed_grad * gain_half[:, columns]
                 hidden_grad = (
@@ -578,6 +584,10 @@
     def _(step):
         sweep(step)
 
+    @pl.when(section > EAGER)
+    def _():
+        turn_over()
+
     @pl.when(jnp.logical_not(has_after))
     def _():
         @pl.loop(0, entries)
@@ -602,6 +612,10 @@
     @pl.loop(first_stop, blocks)
     def _(step):
         sweep(step)
+
+    @pl.when(section == EAGER)
+    def _():
+        turn_over()
 
     @pl.when(has_after)
     def _():
@@ -744,7 +758,7 @@
     feature_width = input_map.shape[0]
     signal_width = output_map_small.shape[0]
     asked = queries.shape[0]
-    chunks, tiles = 4, 2
+    chunks, tiles = 2, 4
     events = len(gather_events(count))
     stretches = half // (PAIR * rows)
     dma = pltpu.SemaphoreType.DMA
@@ -769,6 +783,7 @@
             pltpu.VMEM((1, asked), queries.dtype),
             dma((5,)),
             pltpu.VMEM((2, half, value_width), jnp.bfloat16),
+            pltpu.VMEM((value_width, half), jnp.bfloat16),
             pltpu.VMEM((size, size), jnp.float32),
             pltpu.VMEM((BLOCK, size), jnp.float32),
             pltpu.VMEM((BLOCK, BLOCK), jnp.float32),

time: 193 us -> 192 us (level)
  no operation moved by 1% of the time
where the time goes in v5:
time: 192 us
  Pallas kernels  191 us (99%)
    pallas_call x1, Pallas kernels, window(): pl.pallas_call(functools.partial(window_kernel, sections, count), out_sha...  191 us

profile of v5, /device:TPU:0, one launch (start us, length us, event | category | flops | bytes accessed | tf_op | source)
XLA Modules:
  0.0 191.9 jit_solution(1151486574213954625)
XLA Ops:
  0.0 190.6 %window.1 = f32[2,16]{1,0:T(2,128)} custom-call(bf16[2,96,4096]{2,1,0:T(8,128)(2,1)} %bitcast.10, bf16[2,96,4096]{2,1,0:T(8,128)(2,1)} %bitcast.11, bf16[1,4096]{1,0:T(2,128)(2,1)} %gain_kept.1, s32[1,2]{1,0:T(1,128)} %bitcast.16, bf16[512,1024]{1,0:T(8,128)(2,1)} %bitcast.12, bf16[512,1024]{1,0:T(8,128)(2,1)} %bitcast.13, bf16[32,4096]{1,0:T(8,128)(2,1)} %bitcast.14, ...), custom_call_target="tpu_custom_call" | custom-call | tf_op jit(solution)/shard_map/window/pallas_call | solution.py:770
  190.6 1.2 copy.12
